TPU v7x, 512 devices: a whole 4x4x16 slice. The times are simulated.
512 devices in a mesh: dp: 4 (over y_lo, core), tp: 128 (over z, x, y_hi).
Axes of the slice: x: 4, y: 4 (y_hi: 2, y_lo: 2; y = y_hi * 2 + y_lo), z: 16, core: 2. Of those that a mesh axis runs over, the one named last changes fastest.
Arguments:
- inputs: bfloat16 [4, 128, 8192], P('dp', 'tp'), may hold values from -134 to 134, as said below
- norm_gain: float32 [8192], replicated, may hold values from 0.1 to 1.9
- gate_grad: bfloat16 [4, 128, 16384], P('dp', None, 'tp'), may hold values from -36 to 36
- up_grad: bfloat16 [4, 128, 16384], P('dp', None, 'tp'), may hold values from -36 to 36
- gate_weight: bfloat16 [8192, 16384], P(None, 'tp'), may hold values from -0.046875 to 0.046875
- up_weight: bfloat16 [8192, 16384], P(None, 'tp'), may hold values from -0.046875 to 0.046875
Outputs:
- input_grad: bfloat16 [4, 128, 8192], P('dp', 'tp')
- gain_grad: float32 [8192], replicated
Inputs may be any that keep to these rules, and one draw needn't show every extreme that they name: `inputs`: activations with token and feature scales.
All inputs are finite; a program needn't handle non-finite values.
Results may differ from a plain program's by a relative error of at most 0.00165.
Values may be sent and summed in bfloat16 or wider, within the bound.
A program may use at most 64 MiB of HBM per device.

v0:
```python
import jax
import jax.numpy as jnp
from jax import lax
from jax.sharding import Mesh
from jax.sharding import PartitionSpec as P

DP_TP = ("dp_0", "dp_1", "tp_0", "tp_1", "tp_2")
TP = ("tp_0", "tp_1", "tp_2")
DP = ("dp_0", "dp_1")


epsilon = 1e-05


def over_axes(x, axes):
    for axis in axes:
        x = lax.psum(x, axis)
    return x


def split_up(x, dim, count):
    before, after = (x.shape[:dim], x.shape[dim + 1 :])
    return jnp.moveaxis(x.reshape(*before, count, -1, *after), dim, 0)


def sent_and_summed(x, axis, dim):
    tiles = split_up(x, dim, lax.axis_size(axis))
    arrived = lax.all_to_all(tiles, axis, split_axis=0, concat_axis=0, tiled=True)
    return arrived.sum(axis=0)


def sum_by_axis(x, axes, dim):
    far, near = axes
    tiles = split_up(x, dim, lax.axis_size(far))
    nearer = sent_and_summed(tiles, near, dim + 1)
    arrived = lax.all_to_all(nearer, far, split_axis=0, concat_axis=0, tiled=True)
    return arrived.sum(axis=0)


def normalize(values):
    inv_rms = lax.rsqrt(jnp.mean(values * values, axis=-1, keepdims=True) + epsilon)
    return (inv_rms, values * inv_rms)


def total_gain(partial_gain):
    return over_axes(partial_gain, DP_TP)


def per_device(inputs, norm_gain, gate_grad, up_grad, gate_weight, up_weight):
    cot_gate = gate_grad[0]
    cot_up = up_grad[0]
    dims = (((1,), (1,)), ((), ()))
    local_rows = inputs[0].astype(jnp.float32)
    inv_rms, normed = normalize(local_rows)
    result = lax.dot_general(cot_gate, gate_weight, dims, preferred_element_type=jnp.float32)
    row_grad = sum_by_axis(
        result + lax.dot_general(cot_up, up_weight, dims, preferred_element_type=jnp.float32),
        (("tp_0", "tp_1"), "tp_2"),
        0,
    )
    gain_grad = total_gain(jnp.sum(row_grad * normed, axis=0))
    scaled = row_grad * norm_gain
    inner = jnp.mean(scaled * normed, axis=-1, keepdims=True)
    input_grad = (inv_rms * (scaled - normed * inner)).astype(jnp.bfloat16)
    return (input_grad[None], gain_grad)


def solution(mesh):
    finer = Mesh(mesh.devices.reshape(2, 2, 16, 4, 2), ("dp_0", "dp_1", "tp_0", "tp_1", "tp_2"))
    return jax.shard_map(
        per_device,
        mesh=finer,
        in_specs=(P(DP, TP, None), P(), P(DP, None, TP), P(DP, None, TP), P(None, TP), P(None, TP)),
        out_specs=(P(DP, TP, None), P()),
        check_vma=False,
    )
```

profile of v0, /device:TPU:16, one launch (start us, length us, event | category | flops | bytes accessed | tf_op | source)
XLA Modules:
  0.0 293.2 jit_solution(13925737791889651203)
XLA Ops:
  0.6 0.0 copy-start
  0.6 0.0 copy-start.1
  0.7 0.0 copy-start.3
  0.7 1.6 copy-done
  2.2 1.5 fusion.1
  3.7 0.0 copy-done.1
  3.7 0.0 copy-done.3
  3.7 2.6 convolution_add_fusion
  6.4 5.8 %reshape_reshape.3 = f32[64,2,1,8192]{3,1,0,2:T(2,128)} reshape(f32[128,8192]{1,0:T(8,128)} %convolution_add_fusion) | data formatting | bytes 8388608 | tf_op jit(solution)/shard_map/reshape;reshape | solution.py:23
  12.2 4.6 %copy.10 = f32[64,2,1,8192]{3,0,2,1:T(8,128)S(1)} copy(f32[64,2,1,8192]{3,1,0,2:T(2,128)} %reshape_reshape.3) | data formatting | bytes 8388608 | tf_op jit(solution)/shard_map/reshape;reshape | solution.py:23
  16.8 50.2 %all_to_all.10 = f32[2,64,1,8192]{3,1,2,0:T(8,128)} all-to-all(f32[2,64,1,8192]{3,1,2,0:T(8,128)S(1)} %bitcast.12), channel_id=1, replica_groups=mesh['dp_0'=2,'dp_1'=2,'tp_0'=16,'tp_1'=4,'tp_2'=2] {'tp_2'}, dimensions={0} | all-to-all | bytes 8388608 | tf_op jit(solution)/shard_map/all_to_all | solution.py:28
  67.0 4.0 %reduce_sum.43 = f32[64,8192]{1,0:T(8,128)} reduce(f32[2,64,1,8192]{3,1,2,0:T(8,128)} %all_to_all.10, f32[]{:T(128)} %constant.8.clone.1), dimensions={0,2}, to_apply=%region_1.0 | reduce | flops 524288 | bytes 6291460 | tf_op jit(solution)/shard_map/reduce_sum | solution.py:29
  71.0 5.3 %reduce_sum.44 = f32[64,1,8192]{2,1,0:T(1,128)} reshape(f32[64,8192]{1,0:T(8,128)} %reduce_sum.43) | data formatting | bytes 4194304 | tf_op jit(solution)/shard_map/reduce_sum | solution.py:29
  76.3 0.0 copy-start.2
  76.3 19.0 %all-to-all-start.1 = ((f32[64,1,8192]{2,1,0:T(1,128)}), f32[64,1,8192]{2,1,0:T(1,128)}, u32[]{:S(2)}, u32[]{:S(2)}) async-start(f32[64,1,8192]{2,1,0:T(1,128)} %reduce_sum.44), calls=%async_computation.1 | async-start | bytes 4194304 | tf_op jit(solution)/shard_map/all_to_all | solution.py:36
  95.3 0.0 copy-done.2
  95.3 0.0 copy-start.4
  95.3 0.7 multiply_reduce_fusion.1
  96.7 97.8 %all-to-all-done.1 = f32[64,1,8192]{2,1,0:T(1,128)} async-done(((f32[64,1,8192]{2,1,0:T(1,128)}), f32[64,1,8192]{2,1,0:T(1,128)}, u32[]{:S(2)}, u32[]{:S(2)}) %all-to-all-start.1) | async-done | bytes 2097184 | tf_op jit(solution)/shard_map/all_to_all | solution.py:36
  194.5 3.4 %reduce_sum.45 = f32[8192]{0:T(1024)S(1)} reduce(f32[64,1,8192]{2,1,0:T(1,128)} %all-to-all-done.1, f32[]{:T(128)} %constant.8.clone.1), dimensions={0,1}, to_apply=%region_2.0 | reduce | flops 516096 | bytes 2129924 | tf_op jit(solution)/shard_map/reduce_sum | solution.py:37
  197.9 0.0 copy-done.4
  197.9 0.6 multiply_reduce_fusion
  199.2 0.6 broadcast_in_dim.2
  199.8 9.0 %psum.35 = f32[8192]{0:T(1024)S(1)} all-reduce(f32[8192]{0:T(1024)S(1)} %get-tuple-element.4), channel_id=1, replica_groups=mesh['dp_0'=2,'dp_1'=2,'tp_0'=16,'tp_1'=4,'tp_2'=2] {'dp_0'}, use_global_device_ids=true, to_apply=%region_4.0 | all-reduce | flops 8192 | bytes 65536 | tf_op jit(solution)/shard_map/psum | solution.py:17
  208.8 3.4 %psum.36 = f32[8192]{0:T(1024)S(1)} all-reduce(f32[8192]{0:T(1024)S(1)} %psum.35), channel_id=1, replica_groups=mesh['dp_0'=2,'dp_1'=2,'tp_0'=16,'tp_1'=4,'tp_2'=2] {'dp_1'}, use_global_device_ids=true, to_apply=%region_5.0 | all-reduce | flops 8192 | bytes 65536 | tf_op jit(solution)/shard_map/psum | solution.py:17
  212.3 52.7 %psum.37 = f32[8192]{0:T(1024)S(1)} all-reduce(f32[8192]{0:T(1024)S(1)} %psum.36), channel_id=1, replica_groups=mesh['dp_0'=2,'dp_1'=2,'tp_0'=16,'tp_1'=4,'tp_2'=2] {'tp_0'}, use_global_device_ids=true, to_apply=%region_6.0 | all-reduce | flops 8192 | bytes 65536 | tf_op jit(solution)/shard_map/psum | solution.py:17
  264.9 17.0 %psum.38 = f32[8192]{0:T(1024)S(1)} all-reduce(f32[8192]{0:T(1024)S(1)} %psum.37), channel_id=1, replica_groups=mesh['dp_0'=2,'dp_1'=2,'tp_0'=16,'tp_1'=4,'tp_2'=2] {'tp_1'}, use_global_device_ids=true, to_apply=%region_7.0 | all-reduce | flops 8192 | bytes 65536 | tf_op jit(solution)/shard_map/psum | solution.py:17
  281.9 11.3 %psum.39 = f32[8192]{0:T(1024)} all-reduce(f32[8192]{0:T(1024)S(1)} %psum.38), channel_id=1, replica_groups=mesh['dp_0'=2,'dp_1'=2,'tp_0'=16,'tp_1'=4,'tp_2'=2] {'tp_2'}, use_global_device_ids=true, to_apply=%region_8.0 | all-reduce | flops 8192 | bytes 65536 | tf_op jit(solution)/shard_map/psum | solution.py:17
  (2 shorter events, 0.0 us)
Async XLA Ops:
  0.6 1.6 copy-start
  0.6 3.1 %copy-start.1 = (bf16[8192,128]{1,0:T(8,128)(2,1)S(1)}, bf16[8192,128]{1,0:T(8,128)(2,1)}, u32[]{:S(2)}) copy-start(bf16[8192,128]{1,0:T(8,128)(2,1)} %param.11) | copy-start | bytes 6291460
  0.7 3.1 %copy-start.3 = (bf16[1,128,128]{2,1,0:T(8,128)(2,1)S(1)}, bf16[1,128,128]{2,1,0:T(8,128)(2,1)}, u32[]{:S(2)}) copy-start(bf16[1,128,128]{2,1,0:T(8,128)(2,1)} %param.9) | copy-start | bytes 98308
  76.3 19.0 %copy-start.2 = (bf16[1,1,8192]{2,1,0:T(2,128)(2,1)S(1)}, bf16[1,1,8192]{2,1,0:T(2,128)(2,1)}, u32[]{:S(2)}) copy-start(bf16[1,1,8192]{2,1,0:T(2,128)(2,1)} %param.6) | copy-start | bytes 49156
  76.3 118.2 %all-to-all-start.1 = ((f32[64,1,8192]{2,1,0:T(1,128)}), f32[64,1,8192]{2,1,0:T(1,128)}, u32[]{:S(2)}, u32[]{:S(2)}) async-start(f32[64,1,8192]{2,1,0:T(1,128)} %reduce_sum.44), calls=%async_computation.1 | async-start | bytes 4194304 | tf_op jit(solution)/shard_map/all_to_all | solution.py:36
  95.3 102.6 %copy-start.4 = (f32[8192]{0:T(1024)S(1)}, f32[8192]{0:T(1024)}, u32[]{:S(2)}) copy-start(f32[8192]{0:T(1024)} %param.7) | copy-start | bytes 98308
where the time goes:
time: 294 us; the launch traced here: 293 us
  blocking collectives  144 us (49%)
  waiting for transfers between devices  97.8 us (33%)
  starting transfers between devices  19 us (6%)
  local copies, waits for them, and re-layouts  17.9 us (6%)
  other arithmetic  8.7 us (3%)
  matrix products  4.1 us (1%)
    all_to_all x1, waiting for transfers between devices, sum_by_axis(): lax.all_to_all(nearer, far, split_axis=0, concat_axis=0, tiled=True)  97.8 us
    psum x5, blocking collectives, over_axes(): x = lax.psum(x, axis)  93.4 us
    all_to_all x1, blocking collectives, sent_and_summed(): lax.all_to_all(tiles, axis, split_axis=0, concat_axis=0, tiled=True)  50.2 us
    all_to_all x1, starting transfers between devices, sum_by_axis(): lax.all_to_all(nearer, far, split_axis=0, concat_axis=0, tiled=True)  19 us
    another operation x2, local copies, waits for them, and re-layouts, split_up(): return jnp.moveaxis(x.reshape(*before, count, -1, *after), dim, 0)  10.4 us
  transfers between devices with their start and end apart: 1, of which 1 were waited for; matrix products, arithmetic and copies ran while one was open for 0% of the time, Pallas kernels for 0%

commit v1 on v0

v1 whole, which is shorter than its diff:
```python
import jax
import jax.numpy as jnp
from jax import lax
from jax.experimental import pallas as pl
from jax.experimental.pallas import tpu as pltpu
from jax.sharding import Mesh
from jax.sharding import PartitionSpec as P

TP = ("tp_0", "tp_1", "tp_2")
DP = ("dp_0", "dp_1")
MESH = pl.DeviceIdType.MESH

epsilon = 1e-05

D = 8192
NX = 4
NZ = 16
PARTS = 16
PW = D // PARTS
CH = 4
CW = PW // CH
X_ORDER = (1, 3, 2)
Z_DIRECT = (1, 2, 3, -1, -2, -3)
Z_RELAY = ((1, 5), (2, 6), (3, 7), (4, 8), (-1, -5), (-2, -6), (-3, -7))
NT = (((1,), (1,)), ((), ()))


def copy_to(src, dst, send, recv, device):
    copy = pltpu.make_async_remote_copy(
        src_ref=src, dst_ref=dst, send_sem=send, recv_sem=recv, device_id=device, device_id_type=MESH
    )
    copy.start()
    return copy


def wait_bytes(ref, sem):
    pltpu.make_async_copy(ref, ref, sem).wait()


def kernel(
    gw, uw, gg, ug, xin, gain, out, gout,
    cots, wst, wb, psend, pown, yr, qz, rdir, rrel, srel, r2, nown, nrecv, trow, rrow, gown, grecv, gsum, gall,
    w_sem, cx_send, cx_recv, cy_send, cy_recv, cc_send, cc_recv, wx_send, wx_recv, y_send, y_recv,
    zd_send, zd_recv, zr_send, zr_recv, z2_send, z2_recv, n_send, n_recv, t_send, t_recv, g_send, g_recv, a_send, a_recv,
):
    lo, co = lax.axis_index("dp_0"), lax.axis_index("dp_1")
    z, x, hi = lax.axis_index("tp_0"), lax.axis_index("tp_1"), lax.axis_index("tp_2")

    def dev(lo=lo, co=co, z=z, x=x, hi=hi):
        return {"dp_0": lo, "dp_1": co, "tp_0": z, "tp_1": x, "tp_2": hi}

    def at_x(r):
        return lax.rem(x + r, NX)

    def at_z(d):
        return lax.rem(z + (d + NZ), NZ)

    side = lax.rem(lo + hi, 2)

    def part(x, side, co):
        return (x * 2 + side) * 2 + co

    def group_peer(j):
        dx, dlo, dco = j // 4, (j // 2) % 2, j % 2
        px, plo, pco = lax.rem(x + dx, NX), lax.rem(lo + dlo, 2), lax.rem(co + dco, 2)
        return dev(lo=plo, co=pco, x=px), part(px, lax.rem(plo + hi, 2), pco), (plo * 2 + pco) * NX + px

    def far_peer(j):
        dz, dhi = j // 2, j % 2
        phi = lax.rem(hi + dhi, 2)
        return dev(lo=lax.rem(lo + dhi, 2), z=lax.rem(z + dz, NZ), hi=phi)

    mine = part(x, side, co)
    me = (lo * 2 + co) * NX + x
    seq = lo * 2 + co
    y_peer = dev(lo=1 - lo)
    core_peer = dev(co=1 - co)
    partner = dev(lo=1 - lo, hi=1 - hi)

    barrier = pltpu.get_barrier_semaphore()
    for j in range(1, 16):
        pl.semaphore_signal(barrier, inc=1, device_id=group_peer(j)[0], device_id_type=MESH)
    for j in range(1, 2 * NZ):
        pl.semaphore_signal(barrier, inc=1, device_id=far_peer(j), device_id_type=MESH)

    staged = []
    for r in X_ORDER + (0,):
        rows = pl.ds(pl.multiple_of(part(at_x(r), side, co) * PW, PW), PW)
        target = wb.at[0] if r == 0 else wst.at[r - 1]
        for i, w in enumerate((gw, uw)):
            copy = pltpu.make_async_copy(w.at[rows], target.at[:, pl.ds(128 * i, 128)], w_sem.at[r, i])
            copy.start()
            staged.append(copy)

    to = lax.broadcasted_iota(jnp.int32, (128, 128), 0)
    token = lax.broadcasted_iota(jnp.int32, (128, 128), 1)
    order = (token == 2 * (to % 64) + to // 64).astype(jnp.float32).astype(jnp.bfloat16)
    for i, c in enumerate((gg, ug)):
        ordered = jnp.dot(order, c[...], preferred_element_type=jnp.float32).astype(jnp.bfloat16)
        for h in range(2):
            cots[0, h, seq, :, 128 * i : 128 * (i + 1)] = ordered[64 * h : 64 * (h + 1)]

    total = jnp.zeros((1, PW), jnp.float32)
    for j in range(PARTS):
        v = xin[:, PW * j : PW * (j + 1)].astype(jnp.float32)
        total = total + v * v
    inv_rms = lax.rsqrt(jnp.sum(total, axis=-1, keepdims=True) / D + epsilon)
    for j in range(PARTS):
        nown[j] = xin[:, PW * j : PW * (j + 1)].astype(jnp.float32) * inv_rms

    pl.semaphore_wait(barrier, 15 + 2 * NZ - 1)

    sends = []
    own = cots.at[0, :, seq]
    for r in X_ORDER:
        sends.append(copy_to(own, cots.at[r, :, seq], cx_send.at[r - 1], cx_recv.at[r - 1], dev(x=at_x(r))))
    sends.append(copy_to(own, own, cy_send.at[0], cy_recv.at[0], y_peer))
    sends.append(copy_to(own, own, cc_send.at[0], cc_recv.at[0], core_peer))
    for i in range(8):
        staged[i].wait()
    for k in range(CH):
        rows = pl.ds(CW * k, CW)
        for r in X_ORDER:
            sends.append(
                copy_to(
                    wst.at[r - 1, rows], wb.at[r, rows], wx_send.at[r - 1, k], wx_recv.at[r - 1, k], dev(x=at_x(r))
                )
            )
    nrecv[me] = nown[mine]
    for j in range(1, 16):
        peer, theirs, _ = group_peer(j)
        copy_to(nown.at[theirs], nrecv.at[me], n_send, n_recv, peer)

    other = (1 - lo) * 2 + co
    for r in X_ORDER:
        block = cots.at[r, :, seq]
        sends[X_ORDER.index(r)].wait_recv()
        sends.append(copy_to(block, block, cy_send.at[r], cy_recv.at[r], y_peer))
        sends.append(copy_to(block, block, cc_send.at[r], cc_recv.at[r], core_peer))
    for r in (0,) + X_ORDER:
        block = cots.at[r, :, other]
        wait_bytes(block, cy_recv.at[r])
        sends.append(copy_to(block, block, cc_send.at[4 + r], cc_recv.at[4 + r], core_peer))
    for r in range(8):
        wait_bytes(cots.at[0, :, 0], cc_recv.at[r])

    def product(h, k):
        acc = jnp.zeros((256, CW), jnp.float32)
        for r in range(NX):
            rows = cots[r, h].reshape(256, 256)
            acc = acc + lax.dot_general(rows, wb[r, CW * k : CW * (k + 1)], NT, preferred_element_type=jnp.float32)
        return acc

    def multiply(k):
        for r in X_ORDER:
            wait_bytes(wb.at[r, pl.ds(CW * k, CW)], wx_recv.at[r - 1, k])
        psend[k] = product(1 - hi, k)
        sends.append(copy_to(psend.at[k], yr.at[k], y_send.at[k], y_recv.at[k], partner))
        pown[k] = product(hi, k)

    def add_y(k):
        wait_bytes(yr.at[k], y_recv.at[k])
        for b in range(NZ):
            for s in range(4):
                rows = slice(s * 64 + b * 4, s * 64 + b * 4 + 4)
                qz[k, b, 4 * s : 4 * s + 4] = pown[k, rows] + yr[k, rows]
        for i, (d, far) in enumerate(Z_RELAY):
            copy_to(qz.at[k, at_z(far)], rrel.at[k, i], zr_send.at[k], zr_recv.at[k], dev(z=at_z(d)))
        for i, d in enumerate(Z_DIRECT):
            copy_to(qz.at[k, at_z(d)], rdir.at[k, i], zd_send.at[k], zd_recv.at[k], dev(z=at_z(d)))

    def relay(k):
        wait_bytes(rrel.at[k], zr_recv.at[k])
        srel[k, 0] = qz[k, at_z(4)] + rrel[k, 0] + rrel[k, 1] + rrel[k, 2] + rrel[k, 3]
        srel[k, 1] = qz[k, at_z(-4)] + rrel[k, 4] + rrel[k, 5] + rrel[k, 6]
        copy_to(srel.at[k, 0], r2.at[k, 0], z2_send.at[k], z2_recv.at[k], dev(z=at_z(4)))
        copy_to(srel.at[k, 1], r2.at[k, 1], z2_send.at[k], z2_recv.at[k], dev(z=at_z(-4)))

    def add_z(k):
        wait_bytes(rdir.at[k], zd_recv.at[k])
        acc = qz[k, z]
        for i in range(6):
            acc = acc + rdir[k, i]
        wait_bytes(r2.at[k], z2_recv.at[k])
        acc = acc + r2[k, 0] + r2[k, 1]
        for i in range(16):
            trow[i, :, CW * k : CW * (k + 1)] = acc[i : i + 1]

    multiply(0)
    multiply(1)
    add_y(0)
    multiply(2)
    add_y(1)
    relay(0)
    multiply(3)
    add_y(2)
    relay(1)
    add_z(0)
    add_y(3)
    relay(2)
    add_z(1)
    relay(3)
    add_z(2)
    add_z(3)

    rrow[mine] = trow[me]
    for j in range(1, 16):
        peer, _, theirs = group_peer(j)
        copy_to(trow.at[theirs], rrow.at[mine], t_send, t_recv, peer)

    wait_bytes(nrecv.at[pl.ds(0, 15)], n_recv)
    acc = trow[0] * nrecv[0]
    for i in range(1, 16):
        acc = acc + trow[i] * nrecv[i]
    gown[...] = acc
    here = z * 2 + hi
    grecv[here] = acc
    for j in range(1, 2 * NZ):
        copy_to(gown, grecv.at[here], g_send, g_recv, far_peer(j))

    wait_bytes(rrow.at[pl.ds(0, 15)], t_recv)
    total = jnp.zeros((1, PW), jnp.float32)
    for j in range(PARTS):
        total = total + rrow[j] * gain[:, PW * j : PW * (j + 1)] * nown[j]
    inner = jnp.sum(total, axis=-1, keepdims=True) / D
    for j in range(PARTS):
        cols = slice(PW * j, PW * (j + 1))
        scaled = rrow[j] * gain[:, cols]
        out[:, cols] = (inv_rms * (scaled - nown[j] * inner)).astype(jnp.bfloat16)

    wait_bytes(grecv.at[pl.ds(0, 2 * NZ - 1)], g_recv)
    acc = grecv[0]
    for i in range(1, 2 * NZ):
        acc = acc + grecv[i]
    gsum[...] = acc
    gall[mine] = acc
    for j in range(1, 16):
        copy_to(gsum, gall.at[mine], a_send, a_recv, group_peer(j)[0])
    wait_bytes(gall.at[pl.ds(0, 15)], a_recv)
    for j in range(PARTS):
        gout[:, PW * j : PW * (j + 1)] = gall[j]

    for copy in sends:
        copy.wait_send()
    for k in range(CH):
        wait_bytes(rdir.at[k], zd_send.at[k])
        wait_bytes(rrel.at[k], zr_send.at[k])
        wait_bytes(r2.at[k], z2_send.at[k])
    wait_bytes(nrecv.at[pl.ds(0, 15)], n_send)
    wait_bytes(rrow.at[pl.ds(0, 15)], t_send)
    wait_bytes(grecv.at[pl.ds(0, 2 * NZ - 1)], g_send)
    wait_bytes(gall.at[pl.ds(0, 15)], a_send)


def per_device(inputs, norm_gain, gate_grad, up_grad, gate_weight, up_weight):
    f32, bf16 = jnp.float32, jnp.bfloat16
    dma = pltpu.SemaphoreType.DMA
    anywhere = pl.BlockSpec(memory_space=pl.ANY)
    vmem = pl.BlockSpec(memory_space=pltpu.VMEM)
    input_grad, gain_grad = pl.pallas_call(
        kernel,
        out_shape=(jax.ShapeDtypeStruct((1, D), bf16), jax.ShapeDtypeStruct((1, D), f32)),
        in_specs=[anywhere, anywhere, vmem, vmem, vmem, vmem],
        out_specs=(vmem, vmem),
        scratch_shapes=[
            pltpu.VMEM((NX, 2, 4, 64, 256), bf16),
            pltpu.VMEM((NX - 1, PW, 256), bf16),
            pltpu.VMEM((NX, PW, 256), bf16),
            pltpu.VMEM((CH, 256, CW), f32),
            pltpu.VMEM((CH, 256, CW), f32),
            pltpu.VMEM((CH, 256, CW), f32),
            pltpu.VMEM((CH, NZ, 16, CW), f32),
            pltpu.VMEM((CH, 6, 16, CW), f32),
            pltpu.VMEM((CH, 7, 16, CW), f32),
            pltpu.VMEM((CH, 2, 16, CW), f32),
            pltpu.VMEM((CH, 2, 16, CW), f32),
            pltpu.VMEM((PARTS, 1, PW), f32),
            pltpu.VMEM((16, 1, PW), f32),
            pltpu.VMEM((16, 1, PW), f32),
            pltpu.VMEM((PARTS, 1, PW), f32),
            pltpu.VMEM((1, PW), f32),
            pltpu.VMEM((2 * NZ, 1, PW), f32),
            pltpu.VMEM((1, PW), f32),
            pltpu.VMEM((PARTS, 1, PW), f32),
            dma((NX, 2)),
            dma((3,)), dma((3,)),
            dma((4,)), dma((4,)),
            dma((8,)), dma((8,)),
            dma((3, CH)), dma((3, CH)),
            dma((CH,)), dma((CH,)),
            dma((CH,)), dma((CH,)),
            dma((CH,)), dma((CH,)),
            dma((CH,)), dma((CH,)),
            dma, dma, dma, dma, dma, dma, dma, dma,
        ],
        compiler_params=pltpu.CompilerParams(collective_id=0, has_side_effects=True, vmem_limit_bytes=24 * 2**20),
    )(
        gate_weight,
        up_weight,
        gate_grad[0],
        up_grad[0],
        inputs[0],
        norm_gain.reshape(1, D),
    )
    return (input_grad[None], gain_grad.reshape(D))


def solution(mesh):
    finer = Mesh(mesh.devices.reshape(2, 2, NZ, NX, 2), ("dp_0", "dp_1", "tp_0", "tp_1", "tp_2"))
    return jax.shard_map(
        per_device,
        mesh=finer,
        in_specs=(P(DP, TP, None), P(), P(DP, None, TP), P(DP, None, TP), P(None, TP), P(None, TP)),
        out_specs=(P(DP, TP, None), P()),
        check_vma=False,
    )
```

time: 294 us -> 77.9 us (0.26)
  the two profiles are of different devices: /device:TPU:16 before, /device:TPU:1 now
where the time goes in v1:
time: 77.9 us; the launch traced here: 77.5 us
  Pallas kernels  69.4 us (89%)
  local copies, waits for them, and re-layouts  7.44 us (10%)
    pallas_call x1, Pallas kernels, per_device(): pl.pallas_call(kernel, out_shape=(jax.ShapeDtypeStruct((1, D), bf16), jax...  69.4 us
    unnamed x14, local copies, waits for them, and re-layouts  7.44 us

profile of v1, /device:TPU:1, one launch (start us, length us, event | category | flops | bytes accessed | tf_op | source)
XLA Modules:
  0.0 77.5 jit_solution(17532012604557676857)
XLA Ops:
  0.6 0.0 copy-start
  0.6 1.6 %copy-done = bf16[8192,128]{1,0:T(8,128)(2,1)S(1)} copy-done((bf16[8192,128]{1,0:T(8,128)(2,1)S(1)}, bf16[8192,128]{1,0:T(8,128)(2,1)}, u32[]{:S(2)}) %copy-start) | copy-done | bytes 2097176
  2.2 0.0 copy-start.1
  2.2 1.6 %copy-done.1 = bf16[8192,128]{1,0:T(8,128)(2,1)S(1)} copy-done((bf16[8192,128]{1,0:T(8,128)(2,1)S(1)}, bf16[8192,128]{1,0:T(8,128)(2,1)}, u32[]{:S(2)}) %copy-start.1) | copy-done | bytes 2097176
  3.8 0.0 copy-start.2
  3.8 0.8 copy-done.2
  4.6 0.0 copy-start.3
  4.6 0.8 copy-done.3
  5.3 0.0 copy-start.4
  5.3 0.8 copy-done.4
  6.1 0.0 copy-start.5
  6.1 0.8 copy-done.5
  6.8 69.4 %shard_map.77 = (bf16[1,8192]{1,0:T(2,128)(2,1)S(1)}, f32[1,8192]{1,0:T(1,128)S(1)}) custom-call(bf16[8192,128]{1,0:T(8,128)(2,1)S(1)} %copy-done, bf16[8192,128]{1,0:T(8,128)(2,1)S(1)} %copy-done.1, bf16[128,128]{1,0:T(8,128)(2,1)S(1)} %bitcast.6, bf16[128,128]{1,0:T(8,128)(2,1)S(1)} %bitcast.7, bf16[1,8192]{1,0:T(2,128)(2,1)S(1)} %bitcast.8, ...), custom_call_target="tpu_custom_call" | custom-call | tf_op jit(solution)/shard_map/pallas_call | solution.py:260
  76.2 0.6 copy.10
  76.9 0.6 copy.11
Async XLA Ops:
  0.6 1.6 %copy-start = (bf16[8192,128]{1,0:T(8,128)(2,1)S(1)}, bf16[8192,128]{1,0:T(8,128)(2,1)}, u32[]{:S(2)}) copy-start(bf16[8192,128]{1,0:T(8,128)(2,1)} %gw.1) | copy-start | bytes 6291460
  2.2 1.6 %copy-start.1 = (bf16[8192,128]{1,0:T(8,128)(2,1)S(1)}, bf16[8192,128]{1,0:T(8,128)(2,1)}, u32[]{:S(2)}) copy-start(bf16[8192,128]{1,0:T(8,128)(2,1)} %uw.1) | copy-start | bytes 6291460
  3.8 0.8 copy-start.2
  4.6 0.8 copy-start.3
  5.3 0.8 copy-start.4
  6.1 0.8 copy-start.5

commit v2 on v1

v2 whole, which is shorter than its diff:
```python
import jax
import jax.numpy as jnp
from jax import lax
from jax.experimental import pallas as pl
from jax.experimental.pallas import tpu as pltpu
from jax.sharding import Mesh
from jax.sharding import PartitionSpec as P

TP = ("tp_0", "tp_1", "tp_2")
DP = ("dp_0", "dp_1")
MESH = pl.DeviceIdType.MESH

epsilon = 1e-05

D = 8192
NX = 4
NZ = 16
PARTS = 16
PW = D // PARTS
CH = 4
CW = PW // CH
X_ORDER = (1, 3, 2)
Z_DIRECT = (1, 2, 3, -1, -2, -3)
Z_RELAY = ((1, 5), (2, 6), (3, 7), (4, 8), (-1, -5), (-2, -6), (-3, -7))
SCHEDULE = (
    ("forward_x", 1),
    ("forward_x", 3),
    ("forward_x", 2),
    ("forward_y", 0),
    ("forward_y", 1),
    ("forward_y", 3),
    ("near", 0),
    ("forward_y", 2),
    ("far", 0),
    ("near", 1),
    ("far", 1),
    ("add_y", 0),
    ("near", 2),
    ("far", 2),
    ("near", 3),
    ("far", 3),
    ("add_y", 1),
    ("relay", 0),
    ("add_y", 2),
    ("relay", 1),
    ("add_y", 3),
    ("add_z", 0),
    ("relay", 2),
    ("add_z", 1),
    ("relay", 3),
    ("add_z", 2),
    ("add_z", 3),
)
NT = (((1,), (1,)), ((), ()))


def copy_to(src, dst, send, recv, device):
    copy = pltpu.make_async_remote_copy(
        src_ref=src, dst_ref=dst, send_sem=send, recv_sem=recv, device_id=device, device_id_type=MESH
    )
    copy.start()
    return copy


def wait_bytes(ref, sem):
    pltpu.make_async_copy(ref, ref, sem).wait()


def kernel(
    gw, uw, gg_in, ug_in, x_in, gain_in, out, gout,
    gg, ug, xin, gain, cots, wst, wb, psend, pown, yr, qz, rdir, rrel, srel, r2, nown, nrecv, trow, rrow, gown, grecv, gsum, gall, gwait,
    k_sem, in_sem, w_sem, cx_send, cx_recv, cy_send, cy_recv, cc_send, cc_recv, wx_send, wx_recv, y_send, y_recv,
    zd_send, zd_recv, zr_send, zr_recv, z2_send, z2_recv, n_send, n_recv, t_send, t_recv, g_send, g_recv, a_send, a_recv,
):
    lo, co = lax.axis_index("dp_0"), lax.axis_index("dp_1")
    z, x, hi = lax.axis_index("tp_0"), lax.axis_index("tp_1"), lax.axis_index("tp_2")

    def dev(lo=lo, co=co, z=z, x=x, hi=hi):
        return {"dp_0": lo, "dp_1": co, "tp_0": z, "tp_1": x, "tp_2": hi}

    def at_x(r):
        return lax.rem(x + r, NX)

    def at_z(d):
        return lax.rem(z + (d + NZ), NZ)

    side = lax.rem(lo + hi, 2)

    def part(x, side, co):
        return (x * 2 + side) * 2 + co

    def group_peer(j):
        dx, dlo, dco = j // 4, (j // 2) % 2, j % 2
        px, plo, pco = lax.rem(x + dx, NX), lax.rem(lo + dlo, 2), lax.rem(co + dco, 2)
        return dev(lo=plo, co=pco, x=px), part(px, lax.rem(plo + hi, 2), pco), (plo * 2 + pco) * NX + px

    def plane_peer(j):
        dx, dlo, dco, dhi = j // 8, (j // 4) % 2, (j // 2) % 2, j % 2
        return dev(lo=lax.rem(lo + dlo, 2), co=lax.rem(co + dco, 2), x=lax.rem(x + dx, NX), hi=lax.rem(hi + dhi, 2))

    def greet(step, d):
        for away in (d, -d):
            pl.semaphore_signal(k_sem.at[step], inc=1, device_id=dev(z=at_z(away)), device_id_type=MESH)

    mine = part(x, side, co)
    me = (lo * 2 + co) * NX + x
    seq = lo * 2 + co
    y_peer = dev(lo=1 - lo)
    core_peer = dev(co=1 - co)
    partner = dev(lo=1 - lo, hi=1 - hi)

    with jax.named_scope("signals"):
        barrier = pltpu.get_barrier_semaphore()
        for j in range(1, 2 * 16):
            pl.semaphore_signal(barrier, inc=1, device_id=plane_peer(j), device_id_type=MESH)
        for away in (1, -1):
            pl.semaphore_signal(barrier, inc=1, device_id=dev(z=at_z(away)), device_id_type=MESH)

    loads = []
    for i, (src, dst) in enumerate(((gg_in, gg), (ug_in, ug), (x_in, xin), (gain_in, gain))):
        copy = pltpu.make_async_copy(src, dst, in_sem.at[i])
        copy.start()
        loads.append(copy)
    staged = []
    for r in X_ORDER + (0,):
        rows = pl.ds(pl.multiple_of(part(at_x(r), side, co) * PW, PW), PW)
        target = wb.at[0] if r == 0 else wst.at[r - 1]
        for i, w in enumerate((gw, uw)):
            copy = pltpu.make_async_copy(w.at[rows], target.at[:, pl.ds(128 * i, 128)], w_sem.at[r, i])
            copy.start()
            staged.append(copy)

    with jax.named_scope("prepare"):
        to = lax.broadcasted_iota(jnp.int32, (128, 128), 0)
        token = lax.broadcasted_iota(jnp.int32, (128, 128), 1)
        order = (token == 2 * (to % 64) + to // 64).astype(jnp.float32).astype(jnp.bfloat16)
        for i, c in enumerate((gg, ug)):
            loads[i].wait()
            ordered = jnp.dot(order, c[...], preferred_element_type=jnp.float32).astype(jnp.bfloat16)
            for h in range(2):
                cots[0, h, seq, :, 128 * i : 128 * (i + 1)] = ordered[64 * h : 64 * (h + 1)]

        loads[2].wait()
        loads[3].wait()
        total = jnp.zeros((1, PW), jnp.float32)
        for j in range(PARTS):
            v = xin[:, PW * j : PW * (j + 1)].astype(jnp.float32)
            total = total + v * v
        inv_rms = lax.rsqrt(jnp.sum(total, axis=-1, keepdims=True) / D + epsilon)
        for j in range(PARTS):
            nown[j] = xin[:, PW * j : PW * (j + 1)].astype(jnp.float32) * inv_rms

    with jax.named_scope("barrier"):
        pl.semaphore_wait(barrier, 31 + 2)
    greet(0, 1)

    sends = []
    with jax.named_scope("start_sends"):
        own = cots.at[0, :, seq]
        for r in X_ORDER:
            sends.append(copy_to(own, cots.at[r, :, seq], cx_send.at[r - 1], cx_recv.at[r - 1], dev(x=at_x(r))))
        sends.append(copy_to(own, own, cy_send.at[0], cy_recv.at[0], y_peer))
        sends.append(copy_to(own, own, cc_send.at[0], cc_recv.at[0], core_peer))
        for i in range(8):
            staged[i].wait()
        for k in range(CH):
            rows = pl.ds(CW * k, CW)
            for r in X_ORDER:
                sends.append(
                    copy_to(
                        wst.at[r - 1, rows], wb.at[r, rows], wx_send.at[r - 1, k], wx_recv.at[r - 1, k], dev(x=at_x(r))
                    )
                )
        nrecv[me] = nown[mine]
        for j in range(1, 16):
            peer, theirs, _ = group_peer(j)
            copy_to(nown.at[theirs], nrecv.at[me], n_send, n_recv, peer)

    other = (1 - lo) * 2 + co

    def forward_x(r):
        block = cots.at[r, :, seq]
        wait_bytes(block, cx_recv.at[r - 1])
        sends.append(copy_to(block, block, cy_send.at[r], cy_recv.at[r], y_peer))
        sends.append(copy_to(block, block, cc_send.at[r], cc_recv.at[r], core_peer))

    def forward_y(r):
        block = cots.at[r, :, other]
        wait_bytes(block, cy_recv.at[r])
        sends.append(copy_to(block, block, cc_send.at[4 + r], cc_recv.at[4 + r], core_peer))

    def product(h, l, k):
        acc = jnp.zeros((128, CW), jnp.float32)
        for r in range(NX):
            rows = cots[r, h, pl.ds(2 * l, 2)].reshape(128, 256)
            acc = acc + lax.dot_general(rows, wb[r, CW * k : CW * (k + 1)], NT, preferred_element_type=jnp.float32)
        return acc

    def multiply(l, b, k):
        if k == 0:
            for r in range(NX):
                wait_bytes(cots.at[0, :, 0], cc_recv.at[4 * b + r])
        if b == 0:
            for r in X_ORDER:
                wait_bytes(wb.at[r, pl.ds(CW * k, CW)], wx_recv.at[r - 1, k])
        psend[k, l] = product(1 - hi, l, k)
        sends.append(copy_to(psend.at[k, l], yr.at[k, l], y_send.at[k, b], y_recv.at[k, b], partner))
        pown[k, l] = product(hi, l, k)

    def multiply_near(k):
        multiply(lo, 0, k)

    def multiply_far(k):
        multiply(1 - lo, 1, k)

    def add_y(k):
        for b in range(2):
            wait_bytes(yr.at[k, 0], y_recv.at[k, b])
        for b in range(NZ):
            for s in range(4):
                rows = slice(s % 2 * 64 + b * 4, s % 2 * 64 + b * 4 + 4)
                qz[k, b, 4 * s : 4 * s + 4] = pown[k, s // 2, rows] + yr[k, s // 2, rows]
        if k == 0:
            pl.semaphore_wait(k_sem.at[1], 2)
            greet(2, 4)
        for i, (d, far) in enumerate(Z_RELAY):
            copy_to(qz.at[k, at_z(far)], rrel.at[k, i], zr_send.at[k], zr_recv.at[k], dev(z=at_z(d)))
        for i, d in enumerate(Z_DIRECT):
            copy_to(qz.at[k, at_z(d)], rdir.at[k, i], zd_send.at[k], zd_recv.at[k], dev(z=at_z(d)))

    def relay(k):
        wait_bytes(rrel.at[k], zr_recv.at[k])
        srel[k, 0] = qz[k, at_z(4)] + rrel[k, 0] + rrel[k, 1] + rrel[k, 2] + rrel[k, 3]
        srel[k, 1] = qz[k, at_z(-4)] + rrel[k, 4] + rrel[k, 5] + rrel[k, 6]
        copy_to(srel.at[k, 0], r2.at[k, 0], z2_send.at[k], z2_recv.at[k], dev(z=at_z(4)))
        copy_to(srel.at[k, 1], r2.at[k, 1], z2_send.at[k], z2_recv.at[k], dev(z=at_z(-4)))

    def add_z(k):
        wait_bytes(rdir.at[k], zd_recv.at[k])
        acc = qz[k, z]
        for i in range(6):
            acc = acc + rdir[k, i]
        wait_bytes(r2.at[k], z2_recv.at[k])
        acc = acc + r2[k, 0] + r2[k, 1]
        for i in range(16):
            trow[i, :, CW * k : CW * (k + 1)] = acc[i : i + 1]

    steps = {
        "forward_x": forward_x,
        "forward_y": forward_y,
        "near": multiply_near,
        "far": multiply_far,
        "add_y": add_y,
        "relay": relay,
        "add_z": add_z,
    }
    for step, k in SCHEDULE:
        with jax.named_scope(f"{step}_{k}"):
            if step == "near" and k == 0:
                pl.semaphore_wait(k_sem.at[0], 2)
                greet(1, 2)
            steps[step](k)

    with jax.named_scope("send_rows"):
        rrow[mine] = trow[me]
        for j in range(1, 16):
            peer, _, theirs = group_peer(j)
            copy_to(trow.at[theirs], rrow.at[mine], t_send, t_recv, peer)

    with jax.named_scope("gain_local"):
        wait_bytes(nrecv.at[pl.ds(0, 15)], n_recv)
        acc = trow[0] * nrecv[0]
        for i in range(1, 16):
            acc = acc + trow[i] * nrecv[i]
        gown[...] = acc
        grecv[z] = acc
        pl.semaphore_wait(k_sem.at[2], 2)
        for j in range(1, NZ):
            copy_to(gown, grecv.at[z], g_send, g_recv, dev(z=at_z(j)))

    with jax.named_scope("gain_far"):
        wait_bytes(grecv.at[pl.ds(0, NZ - 1)], g_recv)
        acc = grecv[0]
        for i in range(1, NZ):
            acc = acc + grecv[i]
        gsum[...] = acc
        gall[hi, mine] = acc
        for j in range(1, 2 * 16):
            copy_to(gsum, gall.at[hi, mine], a_send, a_recv, plane_peer(j))
    with jax.named_scope("rows"):
        wait_bytes(rrow.at[pl.ds(0, 15)], t_recv)
        total = jnp.zeros((1, PW), jnp.float32)
        for j in range(PARTS):
            total = total + rrow[j] * gain[:, PW * j : PW * (j + 1)] * nown[j]
        inner = jnp.sum(total, axis=-1, keepdims=True) / D
        for j in range(PARTS):
            cols = slice(PW * j, PW * (j + 1))
            scaled = rrow[j] * gain[:, cols]
            out[:, cols] = (inv_rms * (scaled - nown[j] * inner)).astype(jnp.bfloat16)

    with jax.named_scope("gain_all"):
        wait_bytes(gwait, a_recv)
        for j in range(PARTS):
            gout[:, PW * j : PW * (j + 1)] = gall[0, j] + gall[1, j]

    with jax.named_scope("drain"):
        for copy in sends:
            copy.wait_send()
        for k in range(CH):
            wait_bytes(rdir.at[k], zd_send.at[k])
            wait_bytes(rrel.at[k], zr_send.at[k])
            wait_bytes(r2.at[k], z2_send.at[k])
        wait_bytes(nrecv.at[pl.ds(0, 15)], n_send)
        wait_bytes(rrow.at[pl.ds(0, 15)], t_send)
        wait_bytes(grecv.at[pl.ds(0, NZ - 1)], g_send)
        wait_bytes(gwait, a_send)


def per_device(inputs, norm_gain, gate_grad, up_grad, gate_weight, up_weight):
    f32, bf16 = jnp.float32, jnp.bfloat16
    dma = pltpu.SemaphoreType.DMA
    hbm = pl.BlockSpec(memory_space=pl.ANY)
    vmem = pl.BlockSpec(memory_space=pltpu.VMEM)
    input_grad, gain_grad = pl.pallas_call(
        kernel,
        out_shape=(jax.ShapeDtypeStruct((1, D), bf16), jax.ShapeDtypeStruct((1, D), f32)),
        in_specs=[hbm] * 6,
        out_specs=(vmem, vmem),
        scratch_shapes=[
            pltpu.VMEM((128, 128), bf16),
            pltpu.VMEM((128, 128), bf16),
            pltpu.VMEM((1, D), bf16),
            pltpu.VMEM((1, D), f32),
            pltpu.VMEM((NX, 2, 4, 64, 256), bf16),
            pltpu.VMEM((NX - 1, PW, 256), bf16),
            pltpu.VMEM((NX, PW, 256), bf16),
            pltpu.VMEM((CH, 2, 128, CW), f32),
            pltpu.VMEM((CH, 2, 128, CW), f32),
            pltpu.VMEM((CH, 2, 128, CW), f32),
            pltpu.VMEM((CH, NZ, 16, CW), f32),
            pltpu.VMEM((CH, 6, 16, CW), f32),
            pltpu.VMEM((CH, 7, 16, CW), f32),
            pltpu.VMEM((CH, 2, 16, CW), f32),
            pltpu.VMEM((CH, 2, 16, CW), f32),
            pltpu.VMEM((PARTS, 1, PW), f32),
            pltpu.VMEM((16, 1, PW), f32),
            pltpu.VMEM((16, 1, PW), f32),
            pltpu.VMEM((PARTS, 1, PW), f32),
            pltpu.VMEM((1, PW), f32),
            pltpu.VMEM((NZ, 1, PW), f32),
            pltpu.VMEM((1, PW), f32),
            pltpu.VMEM((2, PARTS, 1, PW), f32),
            pltpu.VMEM((31, 1, PW), f32),
            pltpu.SemaphoreType.REGULAR((3,)),
            dma((4,)),
            dma((NX, 2)),
            dma((3,)), dma((3,)),
            dma((4,)), dma((4,)),
            dma((8,)), dma((8,)),
            dma((3, CH)), dma((3, CH)),
            dma((CH, 2)), dma((CH, 2)),
            dma((CH,)), dma((CH,)),
            dma((CH,)), dma((CH,)),
            dma((CH,)), dma((CH,)),
            dma, dma, dma, dma, dma, dma, dma, dma,
        ],
        compiler_params=pltpu.CompilerParams(collective_id=0, has_side_effects=True, vmem_limit_bytes=67_043_328),
    )(
        gate_weight,
        up_weight,
        gate_grad[0],
        up_grad[0],
        inputs[0],
        norm_gain.reshape(1, D),
    )
    return (input_grad[None], gain_grad.reshape(D))


def solution(mesh):
    finer = Mesh(mesh.devices.reshape(2, 2, NZ, NX, 2), ("dp_0", "dp_1", "tp_0", "tp_1", "tp_2"))
    return jax.shard_map(
        per_device,
        mesh=finer,
        in_specs=(P(DP, TP, None), P(), P(DP, None, TP), P(DP, None, TP), P(None, TP), P(None, TP)),
        out_specs=(P(DP, TP, None), P()),
        check_vma=False,
    )
```

time: 77.9 us -> 69.4 us (0.89)
  local copies, waits for them, and re-layouts: 7.44 us -> 2.78 us
  Pallas kernels: 69.4 us -> 65.7 us
    unnamed x14 -> x2, local copies, waits for them, and re-layouts: 7.44 us -> 2.78 us
    pallas_call x1, Pallas kernels: 69.4 us -> 65.7 us  [per_device(): pl.pallas_call(kernel, out_shape=(jax.ShapeDtypeStruct((1, D), bf16), jax...]
where the time goes in v2:
time: 69.4 us; the launch traced here: 69.2 us
  Pallas kernels  65.7 us (95%)
  local copies, waits for them, and re-layouts  2.78 us (4%)
    pallas_call x1, Pallas kernels, per_device(): pl.pallas_call(kernel, out_shape=(jax.ShapeDtypeStruct((1, D), bf16), jax...  65.7 us
    unnamed x2, local copies, waits for them, and re-layouts  2.78 us

profile of v2, /device:TPU:1, one launch (start us, length us, event | category | flops | bytes accessed | tf_op | source)
XLA Modules:
  0.0 69.2 jit_solution(3932144187409551070)
XLA Ops:
  0.6 65.7 %shard_map.77 = (bf16[1,8192]{1,0:T(2,128)(2,1)}, f32[1,8192]{1,0:T(1,128)}) custom-call(bf16[8192,128]{1,0:T(8,128)(2,1)} %gw.1, bf16[8192,128]{1,0:T(8,128)(2,1)} %uw.1, bf16[128,128]{1,0:T(8,128)(2,1)} %bitcast.6, bf16[128,128]{1,0:T(8,128)(2,1)} %bitcast.7, bf16[1,8192]{1,0:T(2,128)(2,1)} %bitcast.8, f32[1,8192]{1,0:T(1,128)} %bitcast.9), custom_call_target="tpu_custom_call" | custom-call | tf_op jit(solution)/shard_map/pallas_call | solution.py:324
  66.4 1.4 %copy.10 = bf16[1,1,8192]{2,1,0:T(2,128)(2,1)} copy(bf16[1,1,8192]{2,1,0:T(2,128)(2,1)} %bitcast.11) | data formatting | bytes 32768
  67.8 1.4 %copy.11 = f32[8192]{0:T(1024)} copy(f32[8192]{0:T(1024)} %bitcast.10) | data formatting | bytes 65536

commit v3 on v2

--- a/solution.py
+++ b/solution.py
@@ -21,18 +21,22 @@
 CW = PW // CH
 X_ORDER = (1, 3, 2)
 Z_DIRECT = (1, 2, 3, -1, -2, -3)
-Z_RELAY = ((1, 5), (2, 6), (3, 7), (4, 8), (-1, -5), (-2, -6), (-3, -7))
+Z_UP, Z_DOWN = ((1, 5), (2, 6), (3, 7)), ((-1, -5), (-2, -6), (-3, -7))
+Z_RELAY = (Z_UP + ((4, 8),) + Z_DOWN, Z_DOWN + ((-4, -8),) + Z_UP)
+XW = PW + 128
 SCHEDULE = (
     ("forward_x", 1),
     ("forward_x", 3),
     ("forward_x", 2),
     ("forward_y", 0),
+    ("gather", 0),
     ("forward_y", 1),
     ("forward_y", 3),
     ("near", 0),
     ("forward_y", 2),
     ("far", 0),
     ("near", 1),
+    ("gather_on", 0),
     ("far", 1),
     ("add_y", 0),
     ("near", 2),
@@ -41,13 +45,16 @@
     ("far", 3),
     ("add_y", 1),
     ("relay", 0),
+    ("normalize", 0),
     ("add_y", 2),
     ("relay", 1),
     ("add_y", 3),
+    ("gain_local", 0),
     ("add_z", 0),
     ("relay", 2),
     ("add_z", 1),
     ("relay", 3),
+    ("gain_far", 0),
     ("add_z", 2),
     ("add_z", 3),
 )
@@ -68,9 +75,9 @@
 
 def kernel(
     gw, uw, gg_in, ug_in, x_in, gain_in, out, gout,
-    gg, ug, xin, gain, cots, wst, wb, psend, pown, yr, qz, rdir, rrel, srel, r2, nown, nrecv, trow, rrow, gown, grecv, gsum, gall, gwait,
+    gg, ug, xin, gain, cots, wst, wb, psend, pown, yr, qz, rdir, rrel, srel, r2, nown, xsend, nrecv, xf, xz, nz, trow, rrow, gown, grecv, gsum, gall, gwait,
     k_sem, in_sem, w_sem, cx_send, cx_recv, cy_send, cy_recv, cc_send, cc_recv, wx_send, wx_recv, y_send, y_recv,
-    zd_send, zd_recv, zr_send, zr_recv, z2_send, z2_recv, n_send, n_recv, t_send, t_recv, g_send, g_recv, a_send, a_recv,
+    zd_send, zd_recv, zr_send, zr_recv, z2_send, z2_recv, n_send, n_recv, v_send, v_recv, f_recv, t_send, t_recv, g_send, g_recv, a_send, a_recv,
 ):
     lo, co = lax.axis_index("dp_0"), lax.axis_index("dp_1")
     z, x, hi = lax.axis_index("tp_0"), lax.axis_index("tp_1"), lax.axis_index("tp_2")
@@ -148,7 +155,10 @@
             total = total + v * v
         inv_rms = lax.rsqrt(jnp.sum(total, axis=-1, keepdims=True) / D + epsilon)
         for j in range(PARTS):
-            nown[j] = xin[:, PW * j : PW * (j + 1)].astype(jnp.float32) * inv_rms
+            v = xin[:, PW * j : PW * (j + 1)].astype(jnp.float32)
+            nown[j] = v * inv_rms
+            xsend[j, :, :PW] = v
+            xsend[j, :, PW:] = jnp.broadcast_to(inv_rms, (1, 128))
 
     with jax.named_scope("barrier"):
         pl.semaphore_wait(barrier, 31 + 2)
@@ -161,6 +171,10 @@
             sends.append(copy_to(own, cots.at[r, :, seq], cx_send.at[r - 1], cx_recv.at[r - 1], dev(x=at_x(r))))
         sends.append(copy_to(own, own, cy_send.at[0], cy_recv.at[0], y_peer))
         sends.append(copy_to(own, own, cc_send.at[0], cc_recv.at[0], core_peer))
+        nrecv[me] = xsend[mine]
+        for j in range(1, 16):
+            peer, theirs, _ = group_peer(j)
+            copy_to(xsend.at[theirs], nrecv.at[me], n_send, n_recv, peer)
         for i in range(8):
             staged[i].wait()
         for k in range(CH):
@@ -171,10 +185,6 @@
                         wst.at[r - 1, rows], wb.at[r, rows], wx_send.at[r - 1, k], wx_recv.at[r - 1, k], dev(x=at_x(r))
                     )
                 )
-        nrecv[me] = nown[mine]
-        for j in range(1, 16):
-            peer, theirs, _ = group_peer(j)
-            copy_to(nown.at[theirs], nrecv.at[me], n_send, n_recv, peer)
 
     other = (1 - lo) * 2 + co
 
@@ -220,20 +230,18 @@
             for s in range(4):
                 rows = slice(s % 2 * 64 + b * 4, s % 2 * 64 + b * 4 + 4)
                 qz[k, b, 4 * s : 4 * s + 4] = pown[k, s // 2, rows] + yr[k, s // 2, rows]
-        if k == 0:
-            pl.semaphore_wait(k_sem.at[1], 2)
-            greet(2, 4)
-        for i, (d, far) in enumerate(Z_RELAY):
+        for i, (d, far) in enumerate(Z_RELAY[k % 2]):
             copy_to(qz.at[k, at_z(far)], rrel.at[k, i], zr_send.at[k], zr_recv.at[k], dev(z=at_z(d)))
         for i, d in enumerate(Z_DIRECT):
             copy_to(qz.at[k, at_z(d)], rdir.at[k, i], zd_send.at[k], zd_recv.at[k], dev(z=at_z(d)))
 
     def relay(k):
         wait_bytes(rrel.at[k], zr_recv.at[k])
-        srel[k, 0] = qz[k, at_z(4)] + rrel[k, 0] + rrel[k, 1] + rrel[k, 2] + rrel[k, 3]
-        srel[k, 1] = qz[k, at_z(-4)] + rrel[k, 4] + rrel[k, 5] + rrel[k, 6]
-        copy_to(srel.at[k, 0], r2.at[k, 0], z2_send.at[k], z2_recv.at[k], dev(z=at_z(4)))
-        copy_to(srel.at[k, 1], r2.at[k, 1], z2_send.at[k], z2_recv.at[k], dev(z=at_z(-4)))
+        first = 4 if k % 2 == 0 else -4
+        srel[k, 0] = qz[k, at_z(first)] + rrel[k, 0] + rrel[k, 1] + rrel[k, 2] + rrel[k, 3]
+        srel[k, 1] = qz[k, at_z(-first)] + rrel[k, 4] + rrel[k, 5] + rrel[k, 6]
+        copy_to(srel.at[k, 0], r2.at[k, 0], z2_send.at[k], z2_recv.at[k], dev(z=at_z(first)))
+        copy_to(srel.at[k, 1], r2.at[k, 1], z2_send.at[k], z2_recv.at[k], dev(z=at_z(-first)))
 
     def add_z(k):
         wait_bytes(rdir.at[k], zd_recv.at[k])
@@ -245,7 +253,68 @@
         for i in range(16):
             trow[i, :, CW * k : CW * (k + 1)] = acc[i : i + 1]
 
+    def gather(_):
+        pl.semaphore_wait(k_sem.at[0], 2)
+        greet(1, 2)
+        wait_bytes(nrecv.at[pl.ds(0, 15)], n_recv)
+        for i in range(16):
+            xf[i : i + 1] = nrecv[i]
+        xz[z, :, :PW] = xf[:, :PW].astype(jnp.bfloat16)
+        inv = xf[:, PW:]
+        high = inv.astype(jnp.bfloat16).astype(jnp.float32)
+        middle = (inv - high).astype(jnp.bfloat16).astype(jnp.float32)
+        low = inv - high - middle
+        lane = lax.broadcasted_iota(jnp.int32, (16, 128), 1)
+        split = jnp.where(lane == 0, high, jnp.where(lane == 1, middle, jnp.where(lane == 2, low, 0.0)))
+        xz[z, :, PW:] = split.astype(jnp.bfloat16)
+        pl.semaphore_wait(k_sem.at[1], 2)
+        greet(2, 4)
+        for i, d in enumerate((4, -4)):
+            copy_to(xz.at[z], xz.at[z], v_send, f_recv.at[i], dev(z=at_z(d)))
+        for d in Z_DIRECT:
+            copy_to(xz.at[z], xz.at[z], v_send, v_recv, dev(z=at_z(d)))
+
+    def gather_on(_):
+        for i, (source, targets) in enumerate(((-4, (1, 2, 3, 4)), (4, (-1, -2, -3)))):
+            block = xz.at[at_z(source)]
+            wait_bytes(block, f_recv.at[i])
+            for d in targets:
+                copy_to(block, block, v_send, v_recv, dev(z=at_z(d)))
+
+    def normalize(_):
+        wait_bytes(xz.at[pl.ds(0, 13)], v_recv)
+        for b in range(NZ):
+            block = xz[b].astype(jnp.float32)
+            nz[b] = block[:, :PW] * jnp.sum(block[:, PW:], axis=-1, keepdims=True)
+
+    def gain_local(_):
+        for k in range(CH):
+            cols = slice(CW * k, CW * (k + 1))
+            acc = qz[k, 0] * nz[0, :, cols]
+            for b in range(1, NZ):
+                acc = acc + qz[k, b] * nz[b, :, cols]
+            gown[:, cols] = jnp.sum(acc, axis=0, keepdims=True)
+        grecv[z] = gown[...]
+        pl.semaphore_wait(k_sem.at[2], 2)
+        for j in range(1, NZ):
+            copy_to(gown, grecv.at[z], g_send, g_recv, dev(z=at_z(j)))
+
+    def gain_far(_):
+        wait_bytes(grecv.at[pl.ds(0, NZ - 1)], g_recv)
+        acc = grecv[0]
+        for i in range(1, NZ):
+            acc = acc + grecv[i]
+        gsum[...] = acc
+        gall[hi, mine] = acc
+        for j in range(1, 2 * 16):
+            copy_to(gsum, gall.at[hi, mine], a_send, a_recv, plane_peer(j))
+
     steps = {
+        "gather": gather,
+        "gather_on": gather_on,
+        "normalize": normalize,
+        "gain_local": gain_local,
+        "gain_far": gain_far,
         "forward_x": forward_x,
         "forward_y": forward_y,
         "near": multiply_near,
@@ -256,9 +325,6 @@
     }
     for step, k in SCHEDULE:
         with jax.named_scope(f"{step}_{k}"):
-            if step == "near" and k == 0:
-                pl.semaphore_wait(k_sem.at[0], 2)
-                greet(1, 2)
             steps[step](k)
 
     with jax.named_scope("send_rows"):
@@ -267,26 +333,6 @@
             peer, _, theirs = group_peer(j)
             copy_to(trow.at[theirs], rrow.at[mine], t_send, t_recv, peer)
 
-    with jax.named_scope("gain_local"):
-        wait_bytes(nrecv.at[pl.ds(0, 15)], n_recv)
-        acc = trow[0] * nrecv[0]
-        for i in range(1, 16):
-            acc = acc + trow[i] * nrecv[i]
-        gown[...] = acc
-        grecv[z] = acc
-        pl.semaphore_wait(k_sem.at[2], 2)
-        for j in range(1, NZ):
-            copy_to(gown, grecv.at[z], g_send, g_recv, dev(z=at_z(j)))
-
-    with jax.named_scope("gain_far"):
-        wait_bytes(grecv.at[pl.ds(0, NZ - 1)], g_recv)
-        acc = grecv[0]
-        for i in range(1, NZ):
-            acc = acc + grecv[i]
-        gsum[...] = acc
-        gall[hi, mine] = acc
-        for j in range(1, 2 * 16):
-            copy_to(gsum, gall.at[hi, mine], a_send, a_recv, plane_peer(j))
     with jax.named_scope("rows"):
         wait_bytes(rrow.at[pl.ds(0, 15)], t_recv)
         total = jnp.zeros((1, PW), jnp.float32)
@@ -311,6 +357,7 @@
             wait_bytes(rrel.at[k], zr_send.at[k])
             wait_bytes(r2.at[k], z2_send.at[k])
         wait_bytes(nrecv.at[pl.ds(0, 15)], n_send)
+        wait_bytes(xz.at[pl.ds(0, 15)], v_send)
         wait_bytes(rrow.at[pl.ds(0, 15)], t_send)
         wait_bytes(grecv.at[pl.ds(0, NZ - 1)], g_send)
         wait_bytes(gwait, a_send)
@@ -343,7 +390,11 @@
             pltpu.VMEM((CH, 2, 16, CW), f32),
             pltpu.VMEM((CH, 2, 16, CW), f32),
             pltpu.VMEM((PARTS, 1, PW), f32),
-            pltpu.VMEM((16, 1, PW), f32),
+            pltpu.VMEM((PARTS, 1, XW), f32),
+            pltpu.VMEM((16, 1, XW), f32),
+            pltpu.VMEM((16, XW), f32),
+            pltpu.VMEM((NZ, 16, XW), bf16),
+            pltpu.VMEM((NZ, 16, PW), f32),
             pltpu.VMEM((16, 1, PW), f32),
             pltpu.VMEM((PARTS, 1, PW), f32),
             pltpu.VMEM((1, PW), f32),
@@ -362,7 +413,8 @@
             dma((CH,)), dma((CH,)),
             dma((CH,)), dma((CH,)),
             dma((CH,)), dma((CH,)),
-            dma, dma, dma, dma, dma, dma, dma, dma,
+            dma, dma, dma, dma, dma((2,)),
+            dma, dma, dma, dma, dma, dma,
         ],
         compiler_params=pltpu.CompilerParams(collective_id=0, has_side_effects=True, vmem_limit_bytes=67_043_328),
     )(

time: 69.4 us -> 62.5 us (0.901)
  Pallas kernels: 65.7 us -> 58.8 us
    pallas_call x1, Pallas kernels: 65.7 us -> 58.8 us  [per_device(): pl.pallas_call(kernel, out_shape=(jax.ShapeDtypeStruct((1, D), bf16), jax...]
where the time goes in v3:
time: 62.5 us; the launch traced here: 62.3 us
  Pallas kernels  58.8 us (94%)
  local copies, waits for them, and re-layouts  2.78 us (4%)
  between operations  0.64 us (1%)
    pallas_call x1, Pallas kernels, per_device(): pl.pallas_call(kernel, out_shape=(jax.ShapeDtypeStruct((1, D), bf16), jax...  58.8 us
    unnamed x2, local copies, waits for them, and re-layouts  2.78 us

profile of v3, /device:TPU:1, one launch (start us, length us, event | category | flops | bytes accessed | tf_op | source)
XLA Modules:
  0.0 62.3 jit_solution(5635614293945439835)
XLA Ops:
  0.6 58.8 %shard_map.77 = (bf16[1,8192]{1,0:T(2,128)(2,1)}, f32[1,8192]{1,0:T(1,128)}) custom-call(bf16[8192,128]{1,0:T(8,128)(2,1)} %gw.1, bf16[8192,128]{1,0:T(8,128)(2,1)} %uw.1, bf16[128,128]{1,0:T(8,128)(2,1)} %bitcast.6, bf16[128,128]{1,0:T(8,128)(2,1)} %bitcast.7, bf16[1,8192]{1,0:T(2,128)(2,1)} %bitcast.8, f32[1,8192]{1,0:T(1,128)} %bitcast.9), custom_call_target="tpu_custom_call" | custom-call | tf_op jit(solution)/shard_map/pallas_call | solution.py:371
  59.5 1.4 %copy.10 = bf16[1,1,8192]{2,1,0:T(2,128)(2,1)} copy(bf16[1,1,8192]{2,1,0:T(2,128)(2,1)} %bitcast.11) | data formatting | bytes 32768
  60.9 1.4 %copy.11 = f32[8192]{0:T(1024)} copy(f32[8192]{0:T(1024)} %bitcast.10) | data formatting | bytes 65536

commit v4 on v3

--- a/solution.py
+++ b/solution.py
@@ -20,6 +20,8 @@
 CH = 4
 CW = PW // CH
 X_ORDER = (1, 3, 2)
+LEVELS = 240.0
+MIDDLE = 120.0
 Z_DIRECT = (1, 2, 3, -1, -2, -3)
 Z_UP, Z_DOWN = ((1, 5), (2, 6), (3, 7)), ((-1, -5), (-2, -6), (-3, -7))
 Z_RELAY = (Z_UP + ((4, 8),) + Z_DOWN, Z_DOWN + ((-4, -8),) + Z_UP)
@@ -31,8 +33,8 @@
     ("forward_y", 0),
     ("gather", 0),
     ("forward_y", 1),
+    ("near", 0),
     ("forward_y", 3),
-    ("near", 0),
     ("forward_y", 2),
     ("far", 0),
     ("near", 1),
@@ -69,15 +71,47 @@
     return copy
 
 
+def encode(v):
+    size = jnp.abs(v)
+    top = jnp.maximum(jnp.max(size, axis=-1, keepdims=True) * 1.01, 1e-30)
+    scale = top.astype(jnp.bfloat16).astype(jnp.float32)
+    t = size * (LEVELS / scale)
+    whole = jnp.floor(t)
+    code = jnp.exp2(whole - MIDDLE) * (1.0 + (t - whole))
+    return jnp.where(v < 0.0, -code, code).astype(jnp.bfloat16), scale
+
+
+def decode(code, scale):
+    code = code.astype(jnp.float32)
+    size = jnp.abs(code)
+    power = jnp.floor(jnp.log2(size))
+    t = size * jnp.exp2(-power) + (power + (MIDDLE - 1.0))
+    return jnp.where(code < 0.0, -t, t) * (scale * (1.0 / LEVELS))
+
+
+def eye(rows):
+    row = lax.broadcasted_iota(jnp.int32, (rows, 128), 0)
+    lane = lax.broadcasted_iota(jnp.int32, (rows, 128), 1)
+    return (row == lane).astype(jnp.float32)
+
+
+def as_row(column):
+    return jnp.sum(column * eye(column.shape[0]), axis=0, keepdims=True)
+
+
+def as_column(row, rows):
+    return jnp.sum(row * eye(rows), axis=-1, keepdims=True)
+
+
 def wait_bytes(ref, sem):
     pltpu.make_async_copy(ref, ref, sem).wait()
 
 
 def kernel(
     gw, uw, gg_in, ug_in, x_in, gain_in, out, gout,
-    gg, ug, xin, gain, cots, wst, wb, psend, pown, yr, qz, rdir, rrel, srel, r2, nown, xsend, nrecv, xf, xz, nz, trow, rrow, gown, grecv, gsum, gall, gwait,
+    gg, ug, xin, gain, cots, wst, wb, psend, pown, yr, qz, qc, qs, rdir, rrel, srel, r2, srdir, srrel, ssrel, sr2, nown, xsend, nrecv, xf, xz, nz, trow, rrow, gown, grecv, gsum, gall, gwait,
     k_sem, in_sem, w_sem, cx_send, cx_recv, cy_send, cy_recv, cc_send, cc_recv, wx_send, wx_recv, y_send, y_recv,
-    zd_send, zd_recv, zr_send, zr_recv, z2_send, z2_recv, n_send, n_recv, v_send, v_recv, f_recv, t_send, t_recv, g_send, g_recv, a_send, a_recv,
+    zd_send, zd_recv, zr_send, zr_recv, z2_send, z2_recv, szd_send, szd_recv, szr_send, szr_recv, sz2_send, sz2_recv, n_send, n_recv, v_send, v_recv, f_recv, t_send, t_recv, g_send, g_recv, a_send, a_recv,
 ):
     lo, co = lax.axis_index("dp_0"), lax.axis_index("dp_1")
     z, x, hi = lax.axis_index("tp_0"), lax.axis_index("tp_1"), lax.axis_index("tp_2")
@@ -147,6 +181,17 @@
             for h in range(2):
                 cots[0, h, seq, :, 128 * i : 128 * (i + 1)] = ordered[64 * h : 64 * (h + 1)]
 
+    with jax.named_scope("barrier"):
+        pl.semaphore_wait(barrier, 31 + 2)
+    greet(0, 1)
+
+    sends = []
+    with jax.named_scope("start_sends"):
+        own = cots.at[0, :, seq]
+        for r in X_ORDER:
+            sends.append(copy_to(own, cots.at[r, :, seq], cx_send.at[r - 1], cx_recv.at[r - 1], dev(x=at_x(r))))
+        sends.append(copy_to(own, own, cy_send.at[0], cy_recv.at[0], y_peer))
+        sends.append(copy_to(own, own, cc_send.at[0], cc_recv.at[0], core_peer))
         loads[2].wait()
         loads[3].wait()
         total = jnp.zeros((1, PW), jnp.float32)
@@ -159,18 +204,6 @@
             nown[j] = v * inv_rms
             xsend[j, :, :PW] = v
             xsend[j, :, PW:] = jnp.broadcast_to(inv_rms, (1, 128))
-
-    with jax.named_scope("barrier"):
-        pl.semaphore_wait(barrier, 31 + 2)
-    greet(0, 1)
-
-    sends = []
-    with jax.named_scope("start_sends"):
-        own = cots.at[0, :, seq]
-        for r in X_ORDER:
-            sends.append(copy_to(own, cots.at[r, :, seq], cx_send.at[r - 1], cx_recv.at[r - 1], dev(x=at_x(r))))
-        sends.append(copy_to(own, own, cy_send.at[0], cy_recv.at[0], y_peer))
-        sends.append(copy_to(own, own, cc_send.at[0], cc_recv.at[0], core_peer))
         nrecv[me] = xsend[mine]
         for j in range(1, 16):
             peer, theirs, _ = group_peer(j)
@@ -213,7 +246,9 @@
         if b == 0:
             for r in X_ORDER:
                 wait_bytes(wb.at[r, pl.ds(CW * k, CW)], wx_recv.at[r - 1, k])
-        psend[k, l] = product(1 - hi, l, k)
+        code, scale = encode(product(1 - hi, l, k))
+        psend[k, l, :128] = code
+        psend[k, l, 128:] = jnp.broadcast_to(as_row(scale), (16, 128)).astype(jnp.bfloat16)
         sends.append(copy_to(psend.at[k, l], yr.at[k, l], y_send.at[k, b], y_recv.at[k, b], partner))
         pown[k, l] = product(hi, l, k)
 
@@ -226,30 +261,47 @@
     def add_y(k):
         for b in range(2):
             wait_bytes(yr.at[k, 0], y_recv.at[k, b])
+        for l in range(2):
+            scale = as_column(yr[k, l, 128:129].astype(jnp.float32), 128)
+            pown[k, l] = pown[k, l] + decode(yr[k, l, :128], scale)
         for b in range(NZ):
             for s in range(4):
                 rows = slice(s % 2 * 64 + b * 4, s % 2 * 64 + b * 4 + 4)
-                qz[k, b, 4 * s : 4 * s + 4] = pown[k, s // 2, rows] + yr[k, s // 2, rows]
+                qz[k, b, 4 * s : 4 * s + 4] = pown[k, s // 2, rows]
+        code, scale = encode(qz[k])
+        qc[k] = code
+        qs[k] = jnp.sum(scale * eye(16), axis=1, keepdims=True)
         for i, (d, far) in enumerate(Z_RELAY[k % 2]):
-            copy_to(qz.at[k, at_z(far)], rrel.at[k, i], zr_send.at[k], zr_recv.at[k], dev(z=at_z(d)))
+            copy_to(qc.at[k, at_z(far)], rrel.at[k, i], zr_send.at[k], zr_recv.at[k], dev(z=at_z(d)))
+            copy_to(qs.at[k, at_z(far)], srrel.at[k, i], szr_send.at[k], szr_recv.at[k], dev(z=at_z(d)))
         for i, d in enumerate(Z_DIRECT):
-            copy_to(qz.at[k, at_z(d)], rdir.at[k, i], zd_send.at[k], zd_recv.at[k], dev(z=at_z(d)))
+            copy_to(qc.at[k, at_z(d)], rdir.at[k, i], zd_send.at[k], zd_recv.at[k], dev(z=at_z(d)))
+            copy_to(qs.at[k, at_z(d)], srdir.at[k, i], szd_send.at[k], szd_recv.at[k], dev(z=at_z(d)))
 
     def relay(k):
         wait_bytes(rrel.at[k], zr_recv.at[k])
+        wait_bytes(srrel.at[k], szr_recv.at[k])
         first = 4 if k % 2 == 0 else -4
-        srel[k, 0] = qz[k, at_z(first)] + rrel[k, 0] + rrel[k, 1] + rrel[k, 2] + rrel[k, 3]
-        srel[k, 1] = qz[k, at_z(-first)] + rrel[k, 4] + rrel[k, 5] + rrel[k, 6]
-        copy_to(srel.at[k, 0], r2.at[k, 0], z2_send.at[k], z2_recv.at[k], dev(z=at_z(first)))
-        copy_to(srel.at[k, 1], r2.at[k, 1], z2_send.at[k], z2_recv.at[k], dev(z=at_z(-first)))
+        for i, (d, sources) in enumerate(((first, (0, 1, 2, 3)), (-first, (4, 5, 6)))):
+            acc = qz[k, at_z(d)]
+            for j in sources:
+                acc = acc + decode(rrel[k, j], as_column(srrel[k, j], 16))
+            code, scale = encode(acc)
+            srel[k, i] = code
+            ssrel[k, i] = as_row(scale)
+            copy_to(srel.at[k, i], r2.at[k, i], z2_send.at[k], z2_recv.at[k], dev(z=at_z(d)))
+            copy_to(ssrel.at[k, i], sr2.at[k, i], sz2_send.at[k], sz2_recv.at[k], dev(z=at_z(d)))
 
     def add_z(k):
         wait_bytes(rdir.at[k], zd_recv.at[k])
+        wait_bytes(srdir.at[k], szd_recv.at[k])
         acc = qz[k, z]
         for i in range(6):
-            acc = acc + rdir[k, i]
+            acc = acc + decode(rdir[k, i], as_column(srdir[k, i], 16))
         wait_bytes(r2.at[k], z2_recv.at[k])
-        acc = acc + r2[k, 0] + r2[k, 1]
+        wait_bytes(sr2.at[k], sz2_recv.at[k])
+        for i in range(2):
+            acc = acc + decode(r2[k, i], as_column(sr2[k, i], 16))
         for i in range(16):
             trow[i, :, CW * k : CW * (k + 1)] = acc[i : i + 1]
 
@@ -356,6 +408,9 @@
             wait_bytes(rdir.at[k], zd_send.at[k])
             wait_bytes(rrel.at[k], zr_send.at[k])
             wait_bytes(r2.at[k], z2_send.at[k])
+            wait_bytes(srdir.at[k], szd_send.at[k])
+            wait_bytes(srrel.at[k], szr_send.at[k])
+            wait_bytes(sr2.at[k], sz2_send.at[k])
         wait_bytes(nrecv.at[pl.ds(0, 15)], n_send)
         wait_bytes(xz.at[pl.ds(0, 15)], v_send)
         wait_bytes(rrow.at[pl.ds(0, 15)], t_send)
@@ -381,14 +436,20 @@
             pltpu.VMEM((NX, 2, 4, 64, 256), bf16),
             pltpu.VMEM((NX - 1, PW, 256), bf16),
             pltpu.VMEM((NX, PW, 256), bf16),
+            pltpu.VMEM((CH, 2, 144, CW), bf16),
             pltpu.VMEM((CH, 2, 128, CW), f32),
-            pltpu.VMEM((CH, 2, 128, CW), f32),
-            pltpu.VMEM((CH, 2, 128, CW), f32),
+            pltpu.VMEM((CH, 2, 144, CW), bf16),
             pltpu.VMEM((CH, NZ, 16, CW), f32),
-            pltpu.VMEM((CH, 6, 16, CW), f32),
-            pltpu.VMEM((CH, 7, 16, CW), f32),
-            pltpu.VMEM((CH, 2, 16, CW), f32),
-            pltpu.VMEM((CH, 2, 16, CW), f32),
+            pltpu.VMEM((CH, NZ, 16, CW), bf16),
+            pltpu.VMEM((CH, NZ, 1, 128), f32),
+            pltpu.VMEM((CH, 6, 16, CW), bf16),
+            pltpu.VMEM((CH, 7, 16, CW), bf16),
+            pltpu.VMEM((CH, 2, 16, CW), bf16),
+            pltpu.VMEM((CH, 2, 16, CW), bf16),
+            pltpu.VMEM((CH, 6, 1, 128), f32),
+            pltpu.VMEM((CH, 7, 1, 128), f32),
+            pltpu.VMEM((CH, 2, 1, 128), f32),
+            pltpu.VMEM((CH, 2, 1, 128), f32),
             pltpu.VMEM((PARTS, 1, PW), f32),
             pltpu.VMEM((PARTS, 1, XW), f32),
             pltpu.VMEM((16, 1, XW), f32),
@@ -413,6 +474,9 @@
             dma((CH,)), dma((CH,)),
             dma((CH,)), dma((CH,)),
             dma((CH,)), dma((CH,)),
+            dma((CH,)), dma((CH,)),
+            dma((CH,)), dma((CH,)),
+            dma((CH,)), dma((CH,)),
             dma, dma, dma, dma, dma((2,)),
             dma, dma, dma, dma, dma, dma,
         ],

time: 62.5 us -> 59.2 us (0.947)
  Pallas kernels: 58.8 us -> 55.5 us
    pallas_call x1, Pallas kernels: 58.8 us -> 55.5 us  [per_device(): pl.pallas_call(kernel, out_shape=(jax.ShapeDtypeStruct((1, D), bf16), jax...]
where the time goes in v4:
time: 59.2 us; the launch traced here: 58.9 us
  Pallas kernels  55.5 us (94%)
  local copies, waits for them, and re-layouts  2.78 us (5%)
  between operations  0.64 us (1%)
    pallas_call x1, Pallas kernels, per_device(): pl.pallas_call(kernel, out_shape=(jax.ShapeDtypeStruct((1, D), bf16), jax...  55.5 us
    unnamed x2, local copies, waits for them, and re-layouts  2.78 us

profile of v4, /device:TPU:1, one launch (start us, length us, event | category | flops | bytes accessed | tf_op | source)
XLA Modules:
  0.0 58.9 jit_solution(522138543465103442)
XLA Ops:
  0.6 55.5 %shard_map.77 = (bf16[1,8192]{1,0:T(2,128)(2,1)}, f32[1,8192]{1,0:T(1,128)}) custom-call(bf16[8192,128]{1,0:T(8,128)(2,1)} %gw.1, bf16[8192,128]{1,0:T(8,128)(2,1)} %uw.1, bf16[128,128]{1,0:T(8,128)(2,1)} %bitcast.6, bf16[128,128]{1,0:T(8,128)(2,1)} %bitcast.7, bf16[1,8192]{1,0:T(2,128)(2,1)} %bitcast.8, f32[1,8192]{1,0:T(1,128)} %bitcast.9), custom_call_target="tpu_custom_call" | custom-call | tf_op jit(solution)/shard_map/pallas_call | solution.py:426
  56.1 1.4 %copy.10 = bf16[1,1,8192]{2,1,0:T(2,128)(2,1)} copy(bf16[1,1,8192]{2,1,0:T(2,128)(2,1)} %bitcast.11) | data formatting | bytes 32768
  57.5 1.4 %copy.11 = f32[8192]{0:T(1024)} copy(f32[8192]{0:T(1024)} %bitcast.10) | data formatting | bytes 65536

commit v5 on v4

--- a/solution.py
+++ b/solution.py
@@ -20,6 +20,7 @@
 CH = 4
 CW = PW // CH
 X_ORDER = (1, 3, 2)
+VMEM_GRANT = 55150 * 1024
 LEVELS = 240.0
 MIDDLE = 120.0
 Z_DIRECT = (1, 2, 3, -1, -2, -3)
@@ -27,37 +28,41 @@
 Z_RELAY = (Z_UP + ((4, 8),) + Z_DOWN, Z_DOWN + ((-4, -8),) + Z_UP)
 XW = PW + 128
 SCHEDULE = (
+    ("gather", 0),
     ("forward_x", 1),
     ("forward_x", 3),
     ("forward_x", 2),
     ("forward_y", 0),
-    ("gather", 0),
     ("forward_y", 1),
     ("near", 0),
     ("forward_y", 3),
     ("forward_y", 2),
     ("far", 0),
+    ("own", 0),
+    ("gather_on", 0),
     ("near", 1),
-    ("gather_on", 0),
     ("far", 1),
+    ("own", 1),
     ("add_y", 0),
     ("near", 2),
     ("far", 2),
+    ("own", 2),
     ("near", 3),
     ("far", 3),
+    ("own", 3),
     ("add_y", 1),
+    ("add_y", 2),
     ("relay", 0),
+    ("add_y", 3),
     ("normalize", 0),
-    ("add_y", 2),
+    ("gain_local", 0),
     ("relay", 1),
-    ("add_y", 3),
-    ("gain_local", 0),
+    ("relay", 2),
+    ("relay", 3),
     ("add_z", 0),
-    ("relay", 2),
     ("add_z", 1),
-    ("relay", 3),
+    ("add_z", 2),
     ("gain_far", 0),
-    ("add_z", 2),
     ("add_z", 3),
 )
 NT = (((1,), (1,)), ((), ()))
@@ -150,6 +155,11 @@
     core_peer = dev(co=1 - co)
     partner = dev(lo=1 - lo, hi=1 - hi)
 
+    loads = []
+    for i, (src, dst) in enumerate(((gg_in, gg), (ug_in, ug), (x_in, xin), (gain_in, gain))):
+        copy = pltpu.make_async_copy(src, dst, in_sem.at[i])
+        copy.start()
+        loads.append(copy)
     with jax.named_scope("signals"):
         barrier = pltpu.get_barrier_semaphore()
         for j in range(1, 2 * 16):
@@ -157,11 +167,6 @@
         for away in (1, -1):
             pl.semaphore_signal(barrier, inc=1, device_id=dev(z=at_z(away)), device_id_type=MESH)
 
-    loads = []
-    for i, (src, dst) in enumerate(((gg_in, gg), (ug_in, ug), (x_in, xin), (gain_in, gain))):
-        copy = pltpu.make_async_copy(src, dst, in_sem.at[i])
-        copy.start()
-        loads.append(copy)
     staged = []
     for r in X_ORDER + (0,):
         rows = pl.ds(pl.multiple_of(part(at_x(r), side, co) * PW, PW), PW)
@@ -181,17 +186,6 @@
             for h in range(2):
                 cots[0, h, seq, :, 128 * i : 128 * (i + 1)] = ordered[64 * h : 64 * (h + 1)]
 
-    with jax.named_scope("barrier"):
-        pl.semaphore_wait(barrier, 31 + 2)
-    greet(0, 1)
-
-    sends = []
-    with jax.named_scope("start_sends"):
-        own = cots.at[0, :, seq]
-        for r in X_ORDER:
-            sends.append(copy_to(own, cots.at[r, :, seq], cx_send.at[r - 1], cx_recv.at[r - 1], dev(x=at_x(r))))
-        sends.append(copy_to(own, own, cy_send.at[0], cy_recv.at[0], y_peer))
-        sends.append(copy_to(own, own, cc_send.at[0], cc_recv.at[0], core_peer))
         loads[2].wait()
         loads[3].wait()
         total = jnp.zeros((1, PW), jnp.float32)
@@ -204,10 +198,22 @@
             nown[j] = v * inv_rms
             xsend[j, :, :PW] = v
             xsend[j, :, PW:] = jnp.broadcast_to(inv_rms, (1, 128))
+
+    with jax.named_scope("barrier"):
+        pl.semaphore_wait(barrier, 31 + 2)
+    greet(0, 1)
+
+    sends = []
+    with jax.named_scope("start_sends"):
         nrecv[me] = xsend[mine]
         for j in range(1, 16):
             peer, theirs, _ = group_peer(j)
             copy_to(xsend.at[theirs], nrecv.at[me], n_send, n_recv, peer)
+        own = cots.at[0, :, seq]
+        for r in X_ORDER:
+            sends.append(copy_to(own, cots.at[r, :, seq], cx_send.at[r - 1], cx_recv.at[r - 1], dev(x=at_x(r))))
+        sends.append(copy_to(own, own, cy_send.at[0], cy_recv.at[0], y_peer))
+        sends.append(copy_to(own, own, cc_send.at[0], cc_recv.at[0], core_peer))
         for i in range(8):
             staged[i].wait()
         for k in range(CH):
@@ -232,10 +238,11 @@
         wait_bytes(block, cy_recv.at[r])
         sends.append(copy_to(block, block, cc_send.at[4 + r], cc_recv.at[4 + r], core_peer))
 
-    def product(h, l, k):
-        acc = jnp.zeros((128, CW), jnp.float32)
+    def product(block, k):
+        acc = 0.0
         for r in range(NX):
-            rows = cots[r, h, pl.ds(2 * l, 2)].reshape(128, 256)
+            rows = block(r)
+            rows = rows.reshape(rows.shape[0] * 64, 256)
             acc = acc + lax.dot_general(rows, wb[r, CW * k : CW * (k + 1)], NT, preferred_element_type=jnp.float32)
         return acc
 
@@ -246,28 +253,31 @@
         if b == 0:
             for r in X_ORDER:
                 wait_bytes(wb.at[r, pl.ds(CW * k, CW)], wx_recv.at[r - 1, k])
-        code, scale = encode(product(1 - hi, l, k))
+        code, scale = encode(product(lambda r: cots[r, 1 - hi, pl.ds(2 * l, 2)], k))
         psend[k, l, :128] = code
         psend[k, l, 128:] = jnp.broadcast_to(as_row(scale), (16, 128)).astype(jnp.bfloat16)
         sends.append(copy_to(psend.at[k, l], yr.at[k, l], y_send.at[k, b], y_recv.at[k, b], partner))
-        pown[k, l] = product(hi, l, k)
 
     def multiply_near(k):
         multiply(lo, 0, k)
 
     def multiply_far(k):
         multiply(1 - lo, 1, k)
+
+    def multiply_own(k):
+        pown[k] = product(lambda r: cots[r, hi], k)
 
     def add_y(k):
         for b in range(2):
             wait_bytes(yr.at[k, 0], y_recv.at[k, b])
         for l in range(2):
             scale = as_column(yr[k, l, 128:129].astype(jnp.float32), 128)
-            pown[k, l] = pown[k, l] + decode(yr[k, l, :128], scale)
+            half = slice(128 * l, 128 * (l + 1))
+            pown[k, half] = pown[k, half] + decode(yr[k, l, :128], scale)
         for b in range(NZ):
             for s in range(4):
-                rows = slice(s % 2 * 64 + b * 4, s % 2 * 64 + b * 4 + 4)
-                qz[k, b, 4 * s : 4 * s + 4] = pown[k, s // 2, rows]
+                rows = slice(s * 64 + b * 4, s * 64 + b * 4 + 4)
+                qz[k, b, 4 * s : 4 * s + 4] = pown[k, rows]
         code, scale = encode(qz[k])
         qc[k] = code
         qs[k] = jnp.sum(scale * eye(16), axis=1, keepdims=True)
@@ -371,6 +381,7 @@
         "forward_y": forward_y,
         "near": multiply_near,
         "far": multiply_far,
+        "own": multiply_own,
         "add_y": add_y,
         "relay": relay,
         "add_z": add_z,
@@ -437,7 +448,7 @@
             pltpu.VMEM((NX - 1, PW, 256), bf16),
             pltpu.VMEM((NX, PW, 256), bf16),
             pltpu.VMEM((CH, 2, 144, CW), bf16),
-            pltpu.VMEM((CH, 2, 128, CW), f32),
+            pltpu.VMEM((CH, 256, CW), f32),
             pltpu.VMEM((CH, 2, 144, CW), bf16),
             pltpu.VMEM((CH, NZ, 16, CW), f32),
             pltpu.VMEM((CH, NZ, 16, CW), bf16),
@@ -480,7 +491,7 @@
             dma, dma, dma, dma, dma((2,)),
             dma, dma, dma, dma, dma, dma,
         ],
-        compiler_params=pltpu.CompilerParams(collective_id=0, has_side_effects=True, vmem_limit_bytes=67_043_328),
+        compiler_params=pltpu.CompilerParams(collective_id=0, has_side_effects=True, vmem_limit_bytes=VMEM_GRANT),
     )(
         gate_weight,
         up_weight,

time: 59.2 us -> 55.6 us (0.939)
  Pallas kernels: 55.5 us -> 53.6 us
  local copies, waits for them, and re-layouts: 2.78 us -> 1.23 us
    pallas_call x1, Pallas kernels: 55.5 us -> 53.6 us  [per_device(): pl.pallas_call(kernel, out_shape=(jax.ShapeDtypeStruct((1, D), bf16), jax...]
    unnamed x2, local copies, waits for them, and re-layouts: 2.78 us -> 1.23 us
where the time goes in v5:
time: 55.6 us; the launch traced here: 55.5 us
  Pallas kernels  53.6 us (96%)
  local copies, waits for them, and re-layouts  1.23 us (2%)
  between operations  0.64 us (1%)
    pallas_call x1, Pallas kernels, per_device(): pl.pallas_call(kernel, out_shape=(jax.ShapeDtypeStruct((1, D), bf16), jax...  53.6 us
    unnamed x2, local copies, waits for them, and re-layouts  1.23 us

profile of v5, /device:TPU:1, one launch (start us, length us, event | category | flops | bytes accessed | tf_op | source)
XLA Modules:
  0.0 55.5 jit_solution(7239589337124930373)
XLA Ops:
  0.6 53.6 %shard_map.77 = (bf16[1,8192]{1,0:T(2,128)(2,1)S(1)}, f32[1,8192]{1,0:T(1,128)S(1)}) custom-call(bf16[8192,128]{1,0:T(8,128)(2,1)} %gw.1, bf16[8192,128]{1,0:T(8,128)(2,1)} %uw.1, bf16[128,128]{1,0:T(8,128)(2,1)} %bitcast.8, bf16[128,128]{1,0:T(8,128)(2,1)} %bitcast.9, bf16[1,8192]{1,0:T(2,128)(2,1)} %bitcast.10, f32[1,8192]{1,0:T(1,128)} %bitcast.11), custom_call_target="tpu_custom_call" | custom-call | tf_op jit(solution)/shard_map/pallas_call | solution.py:437
  54.2 0.6 %copy.10 = bf16[1,1,8192]{2,1,0:T(2,128)(2,1)} copy(bf16[1,1,8192]{2,1,0:T(2,128)(2,1)S(1)} %bitcast.7) | data formatting | bytes 32768
  54.9 0.6 %copy.11 = f32[8192]{0:T(1024)} copy(f32[8192]{0:T(1024)S(1)} %bitcast.6) | data formatting | bytes 65536

commit v6 on v5

v6 whole, which is shorter than its diff:
```python
import math

import jax
import jax.numpy as jnp
from jax import lax
from jax.experimental import pallas as pl
from jax.experimental.pallas import tpu as pltpu
from jax.sharding import Mesh
from jax.sharding import PartitionSpec as P

TP = ("tp_0", "tp_1", "tp_2")
DP = ("dp_0", "dp_1")
MESH = pl.DeviceIdType.MESH

epsilon = 1e-05

D = 8192
NX = 4
NZ = 16
PARTS = 16
PW = D // PARTS
CH = 4
CW = PW // CH
X_ORDER = (1, 3, 2)
VMEM_GRANT = 55150 * 1024
LEVELS = 240.0
UNIT = 512
BLOCK = 9
XBLOCK = 33
MIDDLE = 120.0
Z_DIRECT = (1, 2, 3, -1, -2, -3)
Z_UP, Z_DOWN = ((1, 5), (2, 6), (3, 7)), ((-1, -5), (-2, -6), (-3, -7))
Z_RELAY = (Z_UP + ((4, 8),) + Z_DOWN, Z_DOWN + ((-4, -8),) + Z_UP)
XW = PW + 128
SCHEDULE = (
    ("gather", 0),
    ("forward_x", 1),
    ("forward_x", 3),
    ("forward_x", 2),
    ("forward_y", 0),
    ("forward_y", 1),
    ("near", 0),
    ("forward_y", 3),
    ("forward_y", 2),
    ("far", 0),
    ("own", 0),
    ("gather_on", 0),
    ("near", 1),
    ("far", 1),
    ("own", 1),
    ("add_y", 0),
    ("near", 2),
    ("far", 2),
    ("own", 2),
    ("near", 3),
    ("far", 3),
    ("own", 3),
    ("add_y", 1),
    ("add_y", 2),
    ("relay", 0),
    ("add_y", 3),
    ("normalize", 0),
    ("gain_local", 0),
    ("relay", 1),
    ("relay", 2),
    ("relay", 3),
    ("add_z", 0),
    ("add_z", 1),
    ("add_z", 2),
    ("gain_far", 0),
    ("add_z", 3),
)
NT = (((1,), (1,)), ((), ()))


def encode(v):
    size = jnp.abs(v)
    scale = jnp.maximum(jnp.max(size, axis=-1, keepdims=True) * 1.001, 1e-30)
    t = size * (LEVELS / scale)
    whole = jnp.floor(t)
    code = jnp.exp2(whole - MIDDLE) * (1.0 + (t - whole))
    return jnp.where(v < 0.0, -code, code).astype(jnp.bfloat16), scale


def decode(code, scale):
    code = code.astype(jnp.float32)
    size = jnp.abs(code)
    power = jnp.floor(jnp.log2(size))
    t = size * jnp.exp2(-power) + (power + (MIDDLE - 1.0))
    return jnp.where(code < 0.0, -t, t) * (scale * (1.0 / LEVELS))


def eye(rows):
    row = lax.broadcasted_iota(jnp.int32, (rows, 128), 0)
    lane = lax.broadcasted_iota(jnp.int32, (rows, 128), 1)
    return (row == lane).astype(jnp.float32)


def as_row(column):
    return jnp.sum(column * eye(column.shape[0]), axis=0, keepdims=True)


def as_column(row, rows):
    return jnp.sum(row * eye(rows), axis=-1, keepdims=True)


def wait_bytes(ref, sem):
    pltpu.make_async_copy(ref, ref, sem).wait()


def kernel(
    gw, uw, gg_in, ug_in, x_in, gain_in, out, gout,
    gug, xin, gain, cots, wst, wb, psend, spsend, pown, yr, syr, qz, qc, qs, rdir, rrel, srel, r2, srdir, srrel, ssrel, sr2, nown, xsend, nrecv, xf, xz, iz, nz, trow, rrow, gown, grecv, gsum, gall, units,
    k_sem, in_sem, w_sem, send_sem, cx_recv, cy_recv, cc_recv, wx_recv, y_recv, zr_recv, zd_recv, n_recv, v_recv, f_recv,
    t_recv, g_recv, a_recv,
):
    lo, co = lax.axis_index("dp_0"), lax.axis_index("dp_1")
    z, x, hi = lax.axis_index("tp_0"), lax.axis_index("tp_1"), lax.axis_index("tp_2")

    def dev(lo=lo, co=co, z=z, x=x, hi=hi):
        return {"dp_0": lo, "dp_1": co, "tp_0": z, "tp_1": x, "tp_2": hi}

    def at_x(r):
        return lax.rem(x + r, NX)

    def at_z(d):
        return lax.rem(z + (d + NZ), NZ)

    side = lax.rem(lo + hi, 2)

    def part(x, side, co):
        return (x * 2 + side) * 2 + co

    def group_peer(j):
        dx, dlo, dco = j // 4, (j // 2) % 2, j % 2
        px, plo, pco = lax.rem(x + dx, NX), lax.rem(lo + dlo, 2), lax.rem(co + dco, 2)
        return dev(lo=plo, co=pco, x=px), part(px, lax.rem(plo + hi, 2), pco), (plo * 2 + pco) * NX + px

    def plane_peer(j):
        dx, dlo, dco, dhi = j // 8, (j // 4) % 2, (j // 2) % 2, j % 2
        return dev(lo=lax.rem(lo + dlo, 2), co=lax.rem(co + dco, 2), x=lax.rem(x + dx, NX), hi=lax.rem(hi + dhi, 2))

    def greet(step, d):
        for away in (d, -d):
            pl.semaphore_signal(k_sem.at[step], inc=1, device_id=dev(z=at_z(away)), device_id_type=MESH)

    mine = part(x, side, co)
    me = (lo * 2 + co) * NX + x
    seq = lo * 2 + co
    y_peer = dev(lo=1 - lo)
    core_peer = dev(co=1 - co)
    partner = dev(lo=1 - lo, hi=1 - hi)

    sent = []

    def copy_to(src, dst, recv, device):
        pltpu.make_async_remote_copy(
            src_ref=src, dst_ref=dst, send_sem=send_sem, recv_sem=recv, device_id=device, device_id_type=MESH
        ).start()
        sent.append(math.prod(src.shape) * src.dtype.itemsize // UNIT)

    def wait_units(count, sem):
        wait_bytes(units.at[pl.ds(0, count)], sem)

    loads = []
    pairs = ((gg_in, gug.at[0]), (ug_in, gug.at[1]), (x_in, xin), (gain_in, gain))
    for (src, dst), i in zip(pairs, (0, 0, 1, 2)):
        loads.append(pltpu.make_async_copy(src, dst, in_sem.at[i]))
        loads[-1].start()
    with jax.named_scope("signals"):
        barrier = pltpu.get_barrier_semaphore()
        for j in range(1, 2 * 16):
            pl.semaphore_signal(barrier, inc=1, device_id=plane_peer(j), device_id_type=MESH)
        for away in (1, -1):
            pl.semaphore_signal(barrier, inc=1, device_id=dev(z=at_z(away)), device_id_type=MESH)

    for r in X_ORDER + (0,):
        rows = pl.ds(pl.multiple_of(part(at_x(r), side, co) * PW, PW), PW)
        target = wb.at[0] if r == 0 else wst.at[r - 1]
        for i, w in enumerate((gw, uw)):
            pltpu.make_async_copy(w.at[rows], target.at[:, pl.ds(128 * i, 128)], w_sem).start()

    with jax.named_scope("prepare"):
        to = lax.broadcasted_iota(jnp.int32, (128, 128), 0)
        token = lax.broadcasted_iota(jnp.int32, (128, 128), 1)
        order = (token == 2 * (to % 64) + to // 64).astype(jnp.float32).astype(jnp.bfloat16)
        wait_bytes(gug, in_sem.at[0])
        for i in range(2):
            ordered = jnp.dot(order, gug[i], preferred_element_type=jnp.float32).astype(jnp.bfloat16)
            for h in range(2):
                cots[0, h, seq, :, 128 * i : 128 * (i + 1)] = ordered[64 * h : 64 * (h + 1)]

        loads[2].wait()
        loads[3].wait()
        total = jnp.zeros((1, PW), jnp.float32)
        for j in range(PARTS):
            v = xin[:, PW * j : PW * (j + 1)].astype(jnp.float32)
            total = total + v * v
        inv_rms = lax.rsqrt(jnp.sum(total, axis=-1, keepdims=True) / D + epsilon)
        for j in range(PARTS):
            v = xin[:, PW * j : PW * (j + 1)].astype(jnp.float32)
            nown[j] = v * inv_rms
            xsend[j, :, :PW] = v
            xsend[j, :, PW:] = jnp.broadcast_to(inv_rms, (1, 128))

    with jax.named_scope("barrier"):
        pl.semaphore_wait(barrier, 31 + 2)
    greet(0, 1)

    with jax.named_scope("start_sends"):
        nrecv[me] = xsend[mine]
        for j in range(1, 16):
            peer, theirs, _ = group_peer(j)
            copy_to(xsend.at[theirs], nrecv.at[me], n_recv, peer)
        own = cots.at[0, :, seq]
        for r in X_ORDER:
            copy_to(own, cots.at[r, :, seq], cx_recv.at[r - 1], dev(x=at_x(r)))
        copy_to(own, own, cy_recv.at[0], y_peer)
        copy_to(own, own, cc_recv.at[0], core_peer)
        wait_bytes(wb, w_sem)
        for k in range(CH):
            rows = pl.ds(CW * k, CW)
            for r in X_ORDER:
                copy_to(wst.at[r - 1, rows], wb.at[r, rows], wx_recv.at[k], dev(x=at_x(r)))

    other = (1 - lo) * 2 + co

    def forward_x(r):
        block = cots.at[r, :, seq]
        wait_bytes(block, cx_recv.at[r - 1])
        copy_to(block, block, cy_recv.at[r], y_peer)
        copy_to(block, block, cc_recv.at[0], core_peer)

    def forward_y(r):
        block = cots.at[r, :, other]
        wait_bytes(block, cy_recv.at[r])
        copy_to(block, block, cc_recv.at[1], core_peer)

    def product(block, k):
        acc = 0.0
        for r in range(NX):
            rows = block(r)
            rows = rows.reshape(rows.shape[0] * 64, 256)
            acc = acc + lax.dot_general(rows, wb[r, CW * k : CW * (k + 1)], NT, preferred_element_type=jnp.float32)
        return acc

    def multiply(l, b, k):
        if k == 0:
            wait_bytes(cots.at[:, :, 0], cc_recv.at[b])
        if b == 0:
            wait_bytes(wb.at[pl.ds(0, 3), pl.ds(0, CW)], wx_recv.at[k])
        code, scale = encode(product(lambda r: cots[r, 1 - hi, pl.ds(2 * l, 2)], k))
        psend[k, l] = code
        spsend[k, l] = as_row(scale)
        copy_to(psend.at[k, l], yr.at[k, l], y_recv.at[k], partner)
        copy_to(spsend.at[k, l], syr.at[k, l], y_recv.at[k], partner)

    def multiply_near(k):
        multiply(lo, 0, k)

    def multiply_far(k):
        multiply(1 - lo, 1, k)

    def multiply_own(k):
        pown[k] = product(lambda r: cots[r, hi], k)

    def add_y(k):
        wait_units(2 * (64 + 1), y_recv.at[k])
        for l in range(2):
            scale = as_column(syr[k, l], 128)
            half = slice(128 * l, 128 * (l + 1))
            pown[k, half] = pown[k, half] + decode(yr[k, l], scale)
        for b in range(NZ):
            for s in range(4):
                rows = slice(s * 64 + b * 4, s * 64 + b * 4 + 4)
                qz[k, b, 4 * s : 4 * s + 4] = pown[k, rows]
        code, scale = encode(qz[k])
        qc[k] = code
        qs[k] = jnp.sum(scale * eye(16), axis=1, keepdims=True)
        for i, (d, far) in enumerate(Z_RELAY[k % 2]):
            copy_to(qc.at[k, at_z(far)], rrel.at[k, i], zr_recv.at[k], dev(z=at_z(d)))
            copy_to(qs.at[k, at_z(far)], srrel.at[k, i], zr_recv.at[k], dev(z=at_z(d)))
        for i, d in enumerate(Z_DIRECT):
            copy_to(qc.at[k, at_z(d)], rdir.at[k, i], zd_recv.at[k], dev(z=at_z(d)))
            copy_to(qs.at[k, at_z(d)], srdir.at[k, i], zd_recv.at[k], dev(z=at_z(d)))

    def relay(k):
        wait_units(7 * BLOCK, zr_recv.at[k])
        first = 4 if k % 2 == 0 else -4
        for i, (d, sources) in enumerate(((first, (0, 1, 2, 3)), (-first, (4, 5, 6)))):
            acc = qz[k, at_z(d)]
            for j in sources:
                acc = acc + decode(rrel[k, j], as_column(srrel[k, j], 16))
            code, scale = encode(acc)
            srel[k, i] = code
            ssrel[k, i] = as_row(scale)
            copy_to(srel.at[k, i], r2.at[k, i], zd_recv.at[k], dev(z=at_z(d)))
            copy_to(ssrel.at[k, i], sr2.at[k, i], zd_recv.at[k], dev(z=at_z(d)))

    def add_z(k):
        wait_units(8 * BLOCK, zd_recv.at[k])
        acc = qz[k, z]
        for i in range(6):
            acc = acc + decode(rdir[k, i], as_column(srdir[k, i], 16))
        for i in range(2):
            acc = acc + decode(r2[k, i], as_column(sr2[k, i], 16))
        for i in range(16):
            trow[i, :, CW * k : CW * (k + 1)] = acc[i : i + 1]

    def share(b, sem, d):
        for ref in (xz, iz):
            copy_to(ref.at[b], ref.at[b], sem, dev(z=at_z(d)))

    def gather(_):
        pl.semaphore_wait(k_sem.at[0], 2)
        greet(1, 2)
        wait_bytes(nrecv.at[pl.ds(0, 15)], n_recv)
        for i in range(16):
            xf[i : i + 1] = nrecv[i]
        xz[z] = xf[:, :PW].astype(jnp.bfloat16)
        iz[z] = as_row(xf[:, PW : PW + 1])
        pl.semaphore_wait(k_sem.at[1], 2)
        greet(2, 4)
        for i, d in enumerate((4, -4)):
            share(z, f_recv.at[i], d)
        for d in Z_DIRECT:
            share(z, v_recv, d)

    def gather_on(_):
        for i, (source, targets) in enumerate(((-4, (1, 2, 3, 4)), (4, (-1, -2, -3)))):
            wait_units(XBLOCK, f_recv.at[i])
            for d in targets:
                share(at_z(source), v_recv, d)

    def normalize(_):
        wait_units(13 * XBLOCK, v_recv)
        for b in range(NZ):
            nz[b] = xz[b].astype(jnp.float32) * as_column(iz[b], 16)

    def gain_local(_):
        for k in range(CH):
            cols = slice(CW * k, CW * (k + 1))
            acc = qz[k, 0] * nz[0, :, cols]
            for b in range(1, NZ):
                acc = acc + qz[k, b] * nz[b, :, cols]
            gown[:, cols] = jnp.sum(acc, axis=0, keepdims=True)
        grecv[z] = gown[...]
        pl.semaphore_wait(k_sem.at[2], 2)
        for j in range(1, NZ):
            copy_to(gown, grecv.at[z], g_recv, dev(z=at_z(j)))

    def gain_far(_):
        wait_bytes(grecv.at[pl.ds(0, NZ - 1)], g_recv)
        acc = grecv[0]
        for i in range(1, NZ):
            acc = acc + grecv[i]
        gsum[...] = acc
        gall[hi, mine] = acc
        for j in range(1, 2 * 16):
            copy_to(gsum, gall.at[hi, mine], a_recv, plane_peer(j))

    steps = {
        "gather": gather,
        "gather_on": gather_on,
        "normalize": normalize,
        "gain_local": gain_local,
        "gain_far": gain_far,
        "forward_x": forward_x,
        "forward_y": forward_y,
        "near": multiply_near,
        "far": multiply_far,
        "own": multiply_own,
        "add_y": add_y,
        "relay": relay,
        "add_z": add_z,
    }
    for step, k in SCHEDULE:
        with jax.named_scope(f"{step}_{k}"):
            steps[step](k)

    with jax.named_scope("send_rows"):
        rrow[mine] = trow[me]
        for j in range(1, 16):
            peer, _, theirs = group_peer(j)
            copy_to(trow.at[theirs], rrow.at[mine], t_recv, peer)

    with jax.named_scope("rows"):
        wait_bytes(rrow.at[pl.ds(0, 15)], t_recv)
        total = jnp.zeros((1, PW), jnp.float32)
        for j in range(PARTS):
            total = total + rrow[j] * gain[:, PW * j : PW * (j + 1)] * nown[j]
        inner = jnp.sum(total, axis=-1, keepdims=True) / D
        for j in range(PARTS):
            cols = slice(PW * j, PW * (j + 1))
            scaled = rrow[j] * gain[:, cols]
            out[:, cols] = (inv_rms * (scaled - nown[j] * inner)).astype(jnp.bfloat16)

    with jax.named_scope("gain_all"):
        wait_units(31 * PW * 4 // UNIT, a_recv)
        for j in range(PARTS):
            gout[:, PW * j : PW * (j + 1)] = gall[0, j] + gall[1, j]

    with jax.named_scope("drain"):
        wait_units(sum(sent), send_sem)


def per_device(inputs, norm_gain, gate_grad, up_grad, gate_weight, up_weight):
    f32, bf16 = jnp.float32, jnp.bfloat16
    dma = pltpu.SemaphoreType.DMA
    hbm = pl.BlockSpec(memory_space=pl.ANY)
    vmem = pl.BlockSpec(memory_space=pltpu.VMEM)
    input_grad, gain_grad = pl.pallas_call(
        kernel,
        out_shape=(jax.ShapeDtypeStruct((1, D), bf16), jax.ShapeDtypeStruct((1, D), f32)),
        in_specs=[hbm] * 6,
        out_specs=(vmem, vmem),
        scratch_shapes=[
            pltpu.VMEM((2, 128, 128), bf16),
            pltpu.VMEM((1, D), bf16),
            pltpu.VMEM((1, D), f32),
            pltpu.VMEM((NX, 2, 4, 64, 256), bf16),
            pltpu.VMEM((NX - 1, PW, 256), bf16),
            pltpu.VMEM((NX, PW, 256), bf16),
            pltpu.VMEM((CH, 2, 128, CW), bf16),
            pltpu.VMEM((CH, 2, 1, 128), f32),
            pltpu.VMEM((CH, 256, CW), f32),
            pltpu.VMEM((CH, 2, 128, CW), bf16),
            pltpu.VMEM((CH, 2, 1, 128), f32),
            pltpu.VMEM((CH, NZ, 16, CW), f32),
            pltpu.VMEM((CH, NZ, 16, CW), bf16),
            pltpu.VMEM((CH, NZ, 1, 128), f32),
            pltpu.VMEM((CH, 6, 16, CW), bf16),
            pltpu.VMEM((CH, 7, 16, CW), bf16),
            pltpu.VMEM((CH, 2, 16, CW), bf16),
            pltpu.VMEM((CH, 2, 16, CW), bf16),
            pltpu.VMEM((CH, 6, 1, 128), f32),
            pltpu.VMEM((CH, 7, 1, 128), f32),
            pltpu.VMEM((CH, 2, 1, 128), f32),
            pltpu.VMEM((CH, 2, 1, 128), f32),
            pltpu.VMEM((PARTS, 1, PW), f32),
            pltpu.VMEM((PARTS, 1, XW), f32),
            pltpu.VMEM((16, 1, XW), f32),
            pltpu.VMEM((16, XW), f32),
            pltpu.VMEM((NZ, 16, PW), bf16),
            pltpu.VMEM((NZ, 1, 128), f32),
            pltpu.VMEM((NZ, 16, PW), f32),
            pltpu.VMEM((16, 1, PW), f32),
            pltpu.VMEM((PARTS, 1, PW), f32),
            pltpu.VMEM((1, PW), f32),
            pltpu.VMEM((NZ, 1, PW), f32),
            pltpu.VMEM((1, PW), f32),
            pltpu.VMEM((2, PARTS, 1, PW), f32),
            pltpu.VMEM((6000, 1, 128), f32),
            pltpu.SemaphoreType.REGULAR((3,)),
            dma((3,)),
            dma, dma,
            dma((3,)), dma((4,)), dma((2,)),
            dma((CH,)), dma((CH,)),
            dma((CH,)), dma((CH,)),
            dma, dma, dma((2,)),
            dma, dma, dma,
        ],
        compiler_params=pltpu.CompilerParams(collective_id=0, has_side_effects=True, vmem_limit_bytes=VMEM_GRANT),
    )(
        gate_weight,
        up_weight,
        gate_grad[0],
        up_grad[0],
        inputs[0],
        norm_gain.reshape(1, D),
    )
    return (input_grad[None], gain_grad.reshape(D))


def solution(mesh):
    finer = Mesh(mesh.devices.reshape(2, 2, NZ, NX, 2), ("dp_0", "dp_1", "tp_0", "tp_1", "tp_2"))
    return jax.shard_map(
        per_device,
        mesh=finer,
        in_specs=(P(DP, TP, None), P(), P(DP, None, TP), P(DP, None, TP), P(None, TP), P(None, TP)),
        out_specs=(P(DP, TP, None), P()),
        check_vma=False,
    )
```

time: 55.6 us -> 54.6 us (0.982)
  Pallas kernels: 53.6 us -> 52.6 us
    pallas_call x1, Pallas kernels: 53.6 us -> 52.6 us  [per_device(): pl.pallas_call(kernel, out_shape=(jax.ShapeDtypeStruct((1, D), bf16), jax...]
where the time goes in v6:
time: 54.6 us; the launch traced here: 54.4 us
  Pallas kernels  52.6 us (96%)
  local copies, waits for them, and re-layouts  1.23 us (2%)
  between operations  0.64 us (1%)
    pallas_call x1, Pallas kernels, per_device(): pl.pallas_call(kernel, out_shape=(jax.ShapeDtypeStruct((1, D), bf16), jax...  52.6 us
    unnamed x2, local copies, waits for them, and re-layouts  1.23 us

profile of v6, /device:TPU:1, one launch (start us, length us, event | category | flops | bytes accessed | tf_op | source)
XLA Modules:
  0.0 54.4 jit_solution(1129268207338675712)
XLA Ops:
  0.6 52.6 %shard_map.77 = (bf16[1,8192]{1,0:T(2,128)(2,1)S(1)}, f32[1,8192]{1,0:T(1,128)S(1)}) custom-call(bf16[8192,128]{1,0:T(8,128)(2,1)} %gw.1, bf16[8192,128]{1,0:T(8,128)(2,1)} %uw.1, bf16[128,128]{1,0:T(8,128)(2,1)} %bitcast.8, bf16[128,128]{1,0:T(8,128)(2,1)} %bitcast.9, bf16[1,8192]{1,0:T(2,128)(2,1)} %bitcast.10, f32[1,8192]{1,0:T(1,128)} %bitcast.11), custom_call_target="tpu_custom_call" | custom-call | tf_op jit(solution)/shard_map/pallas_call | solution.py:412
  53.2 0.6 %copy.10 = bf16[1,1,8192]{2,1,0:T(2,128)(2,1)} copy(bf16[1,1,8192]{2,1,0:T(2,128)(2,1)S(1)} %bitcast.7) | data formatting | bytes 32768
  53.8 0.6 %copy.11 = f32[8192]{0:T(1024)} copy(f32[8192]{0:T(1024)S(1)} %bitcast.6) | data formatting | bytes 65536

commit v7 on v6

--- a/solution.py
+++ b/solution.py
@@ -33,20 +33,20 @@
 Z_RELAY = (Z_UP + ((4, 8),) + Z_DOWN, Z_DOWN + ((-4, -8),) + Z_UP)
 XW = PW + 128
 SCHEDULE = (
-    ("gather", 0),
     ("forward_x", 1),
     ("forward_x", 3),
     ("forward_x", 2),
     ("forward_y", 0),
     ("forward_y", 1),
+    ("gather", 0),
+    ("forward_y", 3),
     ("near", 0),
-    ("forward_y", 3),
     ("forward_y", 2),
     ("far", 0),
     ("own", 0),
-    ("gather_on", 0),
     ("near", 1),
     ("far", 1),
+    ("gather_on", 0),
     ("own", 1),
     ("add_y", 0),
     ("near", 2),
@@ -111,7 +111,7 @@
 def kernel(
     gw, uw, gg_in, ug_in, x_in, gain_in, out, gout,
     gug, xin, gain, cots, wst, wb, psend, spsend, pown, yr, syr, qz, qc, qs, rdir, rrel, srel, r2, srdir, srrel, ssrel, sr2, nown, xsend, nrecv, xf, xz, iz, nz, trow, rrow, gown, grecv, gsum, gall, units,
-    k_sem, in_sem, w_sem, send_sem, cx_recv, cy_recv, cc_recv, wx_recv, y_recv, zr_recv, zd_recv, n_recv, v_recv, f_recv,
+    k_sem, m_sem, in_sem, w_sem, send_sem, cx_recv, cy_recv, cc_recv, wx_recv, y_recv, zr_recv, zd_recv, n_recv, v_recv, f_recv,
     t_recv, g_recv, a_recv,
 ):
     lo, co = lax.axis_index("dp_0"), lax.axis_index("dp_1")
@@ -169,10 +169,9 @@
         loads[-1].start()
     with jax.named_scope("signals"):
         barrier = pltpu.get_barrier_semaphore()
-        for j in range(1, 2 * 16):
-            pl.semaphore_signal(barrier, inc=1, device_id=plane_peer(j), device_id_type=MESH)
-        for away in (1, -1):
-            pl.semaphore_signal(barrier, inc=1, device_id=dev(z=at_z(away)), device_id_type=MESH)
+        near = [dev(x=at_x(r)) for r in X_ORDER] + [dev(z=at_z(1)), dev(z=at_z(-1)), y_peer, core_peer, partner]
+        for peer in near:
+            pl.semaphore_signal(barrier, inc=1, device_id=peer, device_id_type=MESH)
 
     for r in X_ORDER + (0,):
         rows = pl.ds(pl.multiple_of(part(at_x(r), side, co) * PW, PW), PW)
@@ -190,6 +189,22 @@
             for h in range(2):
                 cots[0, h, seq, :, 128 * i : 128 * (i + 1)] = ordered[64 * h : 64 * (h + 1)]
 
+    with jax.named_scope("barrier"):
+        pl.semaphore_wait(barrier, len(near))
+
+    def meet(step, *peers):
+        for peer in peers:
+            pl.semaphore_signal(m_sem.at[step], inc=1, device_id=peer, device_id_type=MESH)
+
+    meet(0, y_peer, core_peer)
+    greet(0, 1)
+
+    with jax.named_scope("start_cots"):
+        own = cots.at[0, :, seq]
+        for r in X_ORDER:
+            copy_to(own, cots.at[r, :, seq], cx_recv.at[r - 1], dev(x=at_x(r)))
+        copy_to(own, own, cy_recv.at[0], y_peer)
+        copy_to(own, own, cc_recv.at[0], core_peer)
         loads[2].wait()
         loads[3].wait()
         total = jnp.zeros((1, PW), jnp.float32)
@@ -202,21 +217,17 @@
             nown[j] = v * inv_rms
             xsend[j, :, :PW] = v
             xsend[j, :, PW:] = jnp.broadcast_to(inv_rms, (1, 128))
-
-    with jax.named_scope("barrier"):
-        pl.semaphore_wait(barrier, 31 + 2)
-    greet(0, 1)
-
+    with jax.named_scope("meet"):
+        pl.semaphore_wait(m_sem.at[0], 2)
+        meet(1, y_peer)
+        pl.semaphore_wait(m_sem.at[1], 1)
+        pl.semaphore_wait(k_sem.at[0], 2)
+        greet(1, 2)
     with jax.named_scope("start_sends"):
         nrecv[me] = xsend[mine]
         for j in range(1, 16):
             peer, theirs, _ = group_peer(j)
             copy_to(xsend.at[theirs], nrecv.at[me], n_recv, peer)
-        own = cots.at[0, :, seq]
-        for r in X_ORDER:
-            copy_to(own, cots.at[r, :, seq], cx_recv.at[r - 1], dev(x=at_x(r)))
-        copy_to(own, own, cy_recv.at[0], y_peer)
-        copy_to(own, own, cc_recv.at[0], core_peer)
         wait_bytes(wb, w_sem)
         for k in range(CH):
             rows = pl.ds(CW * k, CW)
@@ -312,8 +323,6 @@
             copy_to(ref.at[b], ref.at[b], sem, dev(z=at_z(d)))
 
     def gather(_):
-        pl.semaphore_wait(k_sem.at[0], 2)
-        greet(1, 2)
         wait_bytes(nrecv.at[pl.ds(0, 15)], n_recv)
         for i in range(16):
             xf[i : i + 1] = nrecv[i]
@@ -452,6 +461,7 @@
             pltpu.VMEM((2, PARTS, 1, PW), f32),
             pltpu.VMEM((6000, 1, 128), f32),
             pltpu.SemaphoreType.REGULAR((3,)),
+            pltpu.SemaphoreType.REGULAR((2,)),
             dma((3,)),
             dma, dma,
             dma((3,)), dma((4,)), dma((2,)),
@@ -469,6 +479,21 @@
         inputs[0],
         norm_gain.reshape(1, D),
     )
+    def put(a, b, c, d, sem):
+        copies = [pltpu.make_async_copy(a, c, sem.at[0]), pltpu.make_async_copy(b, d, sem.at[1])]
+        for copy in copies:
+            copy.start()
+        for copy in copies:
+            copy.wait()
+
+    input_grad, gain_grad = pl.pallas_call(
+        put,
+        out_shape=(jax.ShapeDtypeStruct((1, D), bf16), jax.ShapeDtypeStruct((1, D), f32)),
+        in_specs=[hbm, hbm],
+        out_specs=(hbm, hbm),
+        scratch_shapes=[dma((2,))],
+        compiler_params=pltpu.CompilerParams(vmem_limit_bytes=2**20),
+    )(input_grad, gain_grad)
     return (input_grad[None], gain_grad.reshape(D))
 
 

time: 54.6 us -> 52.5 us (0.962)
  local copies, waits for them, and re-layouts: 1.23 us -> 0 us
  Pallas kernels: 52.6 us -> 51.7 us
    pallas_call x1, Pallas kernels: 52.6 us -> 51.1 us  [per_device(): pl.pallas_call(kernel, out_shape=(jax.ShapeDtypeStruct((1, D), bf16), jax...]
    unnamed x2 -> x0, local copies, waits for them, and re-layouts: 1.23 us -> none
    pallas_call x0 -> x1, Pallas kernels: none -> 0.65 us  [per_device(): pl.pallas_call(put, out_shape=(jax.ShapeDtypeStruct((1, D), bf16), jax.Sh...]
where the time goes in v7:
time: 52.5 us; the launch traced here: 52.4 us
  Pallas kernels  51.7 us (98%)
  between operations  0.64 us (1%)
    pallas_call x1, Pallas kernels, per_device(): pl.pallas_call(kernel, out_shape=(jax.ShapeDtypeStruct((1, D), bf16), jax...  51.1 us

profile of v7, /device:TPU:1, one launch (start us, length us, event | category | flops | bytes accessed | tf_op | source)
XLA Modules:
  0.0 52.4 jit_solution(7723879299110855194)
XLA Ops:
  0.6 51.1 %shard_map.77 = (bf16[1,8192]{1,0:T(2,128)(2,1)S(1)}, f32[1,8192]{1,0:T(1,128)S(1)}) custom-call(bf16[8192,128]{1,0:T(8,128)(2,1)} %gw.1, bf16[8192,128]{1,0:T(8,128)(2,1)} %uw.1, bf16[128,128]{1,0:T(8,128)(2,1)} %bitcast.6, bf16[128,128]{1,0:T(8,128)(2,1)} %bitcast.7, bf16[1,8192]{1,0:T(2,128)(2,1)} %bitcast.8, f32[1,8192]{1,0:T(1,128)} %bitcast.9), custom_call_target="tpu_custom_call" | custom-call | tf_op jit(solution)/shard_map/pallas_call | solution.py:421
  51.7 0.6 %shard_map.78 = (bf16[1,8192]{1,0:T(2,128)(2,1)}, f32[1,8192]{1,0:T(1,128)}) custom-call(bf16[1,8192]{1,0:T(2,128)(2,1)S(1)} %get-tuple-element.6.a, f32[1,8192]{1,0:T(1,128)S(1)} %get-tuple-element.7.b), custom_call_target="tpu_custom_call" | custom-call | tf_op jit(solution)/shard_map/pallas_call | solution.py:489

commit v8 on v7

--- a/solution.py
+++ b/solution.py
@@ -28,9 +28,9 @@
 BLOCK = 9
 XBLOCK = 33
 MIDDLE = 120.0
-Z_DIRECT = (1, 2, 3, -1, -2, -3)
-Z_UP, Z_DOWN = ((1, 5), (2, 6), (3, 7)), ((-1, -5), (-2, -6), (-3, -7))
-Z_RELAY = (Z_UP + ((4, 8),) + Z_DOWN, Z_DOWN + ((-4, -8),) + Z_UP)
+Z_DIRECT = (3, 2, 1, -3, -2, -1)
+Z_UP, Z_DOWN = ((3, 7), (2, 6), (1, 5)), ((-3, -7), (-2, -6), (-1, -5))
+Z_RELAY = (((4, 8),) + Z_UP + Z_DOWN, ((-4, -8),) + Z_DOWN + Z_UP)
 XW = PW + 128
 SCHEDULE = (
     ("forward_x", 1),

time: 52.5 us -> 52.2 us (level)
  no operation moved by 1% of the time
where the time goes in v8:
time: 52.2 us; the launch traced here: 52.1 us
  Pallas kernels  51.4 us (98%)
  between operations  0.64 us (1%)
    pallas_call x1, Pallas kernels, per_device(): pl.pallas_call(kernel, out_shape=(jax.ShapeDtypeStruct((1, D), bf16), jax...  50.8 us

profile of v8, /device:TPU:1, one launch (start us, length us, event | category | flops | bytes accessed | tf_op | source)
XLA Modules:
  0.0 52.1 jit_solution(9184831813556069666)
XLA Ops:
  0.6 50.8 %shard_map.77 = (bf16[1,8192]{1,0:T(2,128)(2,1)S(1)}, f32[1,8192]{1,0:T(1,128)S(1)}) custom-call(bf16[8192,128]{1,0:T(8,128)(2,1)} %gw.1, bf16[8192,128]{1,0:T(8,128)(2,1)} %uw.1, bf16[128,128]{1,0:T(8,128)(2,1)} %bitcast.6, bf16[128,128]{1,0:T(8,128)(2,1)} %bitcast.7, bf16[1,8192]{1,0:T(2,128)(2,1)} %bitcast.8, f32[1,8192]{1,0:T(1,128)} %bitcast.9), custom_call_target="tpu_custom_call" | custom-call | tf_op jit(solution)/shard_map/pallas_call | solution.py:421
  51.4 0.6 %shard_map.78 = (bf16[1,8192]{1,0:T(2,128)(2,1)}, f32[1,8192]{1,0:T(1,128)}) custom-call(bf16[1,8192]{1,0:T(2,128)(2,1)S(1)} %get-tuple-element.6.a, f32[1,8192]{1,0:T(1,128)S(1)} %get-tuple-element.7.b), custom_call_target="tpu_custom_call" | custom-call | tf_op jit(solution)/shard_map/pallas_call | solution.py:489

commit v9 on v8

--- a/solution.py
+++ b/solution.py
@@ -21,13 +21,14 @@
 PW = D // PARTS
 CH = 4
 CW = PW // CH
-X_ORDER = (1, 3, 2)
+X_ORDER = (2, 1, 3)
 VMEM_GRANT = 55150 * 1024
 LEVELS = 240.0
 UNIT = 512
 BLOCK = 9
 XBLOCK = 33
 MIDDLE = 120.0
+Z_FAR_FIRST = (8, 7, 9, 6, 10, 5, 11, 4, 12, 3, 13, 2, 14, 1, 15)
 Z_DIRECT = (3, 2, 1, -3, -2, -1)
 Z_UP, Z_DOWN = ((3, 7), (2, 6), (1, 5)), ((-3, -7), (-2, -6), (-1, -5))
 Z_RELAY = (((4, 8),) + Z_UP + Z_DOWN, ((-4, -8),) + Z_DOWN + Z_UP)
@@ -355,7 +356,7 @@
             gown[:, cols] = jnp.sum(acc, axis=0, keepdims=True)
         grecv[z] = gown[...]
         pl.semaphore_wait(k_sem.at[2], 2)
-        for j in range(1, NZ):
+        for j in Z_FAR_FIRST:
             copy_to(gown, grecv.at[z], g_recv, dev(z=at_z(j)))
 
     def gain_far(_):

time: 52.2 us -> 52.5 us (level)
  no operation moved by 1% of the time
where the time goes in v9:
time: 52.5 us; the launch traced here: 52.4 us
  Pallas kernels  51.7 us (98%)
  between operations  0.64 us (1%)
    pallas_call x1, Pallas kernels, per_device(): pl.pallas_call(kernel, out_shape=(jax.ShapeDtypeStruct((1, D), bf16), jax...  51.1 us

profile of v9, /device:TPU:1, one launch (start us, length us, event | category | flops | bytes accessed | tf_op | source)
XLA Modules:
  0.0 52.4 jit_solution(12403250618385379977)
XLA Ops:
  0.6 51.1 %shard_map.77 = (bf16[1,8192]{1,0:T(2,128)(2,1)S(1)}, f32[1,8192]{1,0:T(1,128)S(1)}) custom-call(bf16[8192,128]{1,0:T(8,128)(2,1)} %gw.1, bf16[8192,128]{1,0:T(8,128)(2,1)} %uw.1, bf16[128,128]{1,0:T(8,128)(2,1)} %bitcast.6, bf16[128,128]{1,0:T(8,128)(2,1)} %bitcast.7, bf16[1,8192]{1,0:T(2,128)(2,1)} %bitcast.8, f32[1,8192]{1,0:T(1,128)} %bitcast.9), custom_call_target="tpu_custom_call" | custom-call | tf_op jit(solution)/shard_map/pallas_call | solution.py:422
  51.7 0.6 %shard_map.78 = (bf16[1,8192]{1,0:T(2,128)(2,1)}, f32[1,8192]{1,0:T(1,128)}) custom-call(bf16[1,8192]{1,0:T(2,128)(2,1)S(1)} %get-tuple-element.6.a, f32[1,8192]{1,0:T(1,128)S(1)} %get-tuple-element.7.b), custom_call_target="tpu_custom_call" | custom-call | tf_op jit(solution)/shard_map/pallas_call | solution.py:490
